TPU v7x, 256 devices: a whole 4x4x8 slice. The times are simulated.
256 devices in a mesh: seq: 16 (over y, x_lo, core), exp: 16 (over z, x_hi).
Axes of the slice: x: 4 (x_hi: 2, x_lo: 2; x = x_hi * 2 + x_lo), y: 4, z: 8, core: 2. Of those that a mesh axis runs over, the one named last changes fastest.
Arguments:
- queries: bfloat16 [4096, 4096], P('seq', 'exp'), may hold values from -6 to 6
- key_rows: bfloat16 [4096, 512], P('seq'), may hold values from -6 to 6
- value_rows: bfloat16 [4096, 512], P('seq'), may hold values from -6 to 6
- sink_logits: float32 [64], P('exp'), may hold values from -2 to 2
- residual: bfloat16 [4096, 2880], P('seq'), may hold values from -6 to 6
- out_weight: bfloat16 [4096, 2880], P('exp'), may hold values from -0.375 to 0.375
- norm_gain: float32 [2880], replicated, may hold values from 0.25 to 1.75
- expert_ids: int32 [4096, 4], P('seq'), may hold values from 0 to 63, all different within a row; in each aligned block of 256 rows (0 to 255, 256 to 511, ...) at most 24 rows name the same one
- route_gates: float32 [4096, 4], P('seq'), may hold values from 0.1 to 0.6
- gate_proj: bfloat16 [64, 2880, 2048], P('seq', None, 'exp'), may hold values from -0.109375 to 0.109375
- up_proj: bfloat16 [64, 2880, 2048], P('seq', None, 'exp'), may hold values from -0.109375 to 0.109375
- down_proj: bfloat16 [64, 2048, 2880], P('seq', 'exp'), may hold values from -0.125 to 0.125
Outputs:
- layer_out: bfloat16 [4096, 2880], P('seq')
Inputs may be any that keep to these rules, and one draw needn't show every extreme that they name: `expert_ids`: each token names 4 different experts. In each slab of 256 tokens no expert is named by more than 24 entries, and that bound is reached.
All inputs are finite; a program needn't handle non-finite values.
Results may differ from a plain program's by a relative error of at most 0.018.
Values may be sent and summed in bfloat16 or wider, within the bound.
A program may use at most 128 MiB of HBM per device.

v0:
```python
import math

import jax
import jax.numpy as jnp
from jax import lax
from jax.sharding import Mesh
from jax.sharding import PartitionSpec as P

HQ = 64
HK = 8
HEAD = 64
TOP = 4
WIN = 128
EXP = ("exp_0", "exp_1")


def passed_along(x, axis, by):
    count = lax.axis_size(axis)
    pairs = [(i, i + by) for i in range(count) if 0 <= i + by < count]
    return lax.ppermute(x, axis, pairs)


def summed_rows(x, axes, dim):
    for axis in axes:
        x = lax.psum_scatter(x, axis, scatter_dimension=dim, tiled=True)
    return x


def side_by_side(arrays, axis, dim, along):
    widths = [a.shape[along] for a in arrays]
    both = jnp.concatenate(arrays, axis=along)
    out = lax.all_gather(both, axis, axis=dim, tiled=True)
    return tuple(jnp.split(out, [sum(widths[:k]) for k in range(1, len(widths))], axis=along))


def from_everyone(x, axis):
    copies = jnp.broadcast_to(x, (lax.axis_size(axis), *x.shape))
    return lax.all_to_all(copies, axis, split_axis=0, concat_axis=0, tiled=True)


def joined_along(pieces, dim):
    pieces = jnp.moveaxis(pieces, 0, dim)
    shape = pieces.shape
    return pieces.reshape(*shape[:dim], shape[dim] * shape[dim + 1], *shape[dim + 2 :])


def gather_directly(x, axis, dim):
    pieces = from_everyone(x, axis)
    return joined_along(pieces, dim)


def normalize(mixed, gain):
    wide_vals = mixed.astype(jnp.float32)
    inv_scale = lax.rsqrt(jnp.mean(wide_vals * wide_vals, axis=-1, keepdims=True) + 1e-05)
    return (wide_vals * inv_scale * gain).astype(jnp.bfloat16)


def activate(gate_acc, up_acc):
    gate_acc = jnp.minimum(gate_acc, 7.0)
    up_acc = jnp.clip(up_acc, -7.0, 7.0)
    return ((up_acc + 1.0) * gate_acc * jax.nn.sigmoid(1.702 * gate_acc)).astype(jnp.bfloat16)


def send_back(partial_out):
    return lax.all_to_all(partial_out, "seq", split_axis=0, concat_axis=0, tiled=True)


def on_device(
    queries,
    key_rows,
    value_rows,
    sink_logits,
    residual,
    out_weight,
    norm_gain,
    expert_ids,
    route_gates,
    gate_proj,
    up_proj,
    down_proj,
):
    tok_rows = queries.shape[0]
    local_heads = queries.shape[1] // HEAD
    per_group = HQ // HK
    column = lax.axis_index(EXP)
    slab_index = lax.axis_index("seq")
    tail_rows = passed_along((key_rows[tok_rows - WIN :], value_rows[tok_rows - WIN :]), "seq", 1)
    key_full = jnp.concatenate([tail_rows[0], key_rows], 0)
    value_full = jnp.concatenate([tail_rows[1], value_rows], 0)
    kv_count = max(1, local_heads // per_group)
    kv_start = column * local_heads // per_group
    key_sel = lax.dynamic_slice_in_dim(key_full, kv_start * HEAD, kv_count * HEAD, 1).reshape(
        WIN + tok_rows, kv_count, HEAD
    )
    value_sel = lax.dynamic_slice_in_dim(value_full, kv_start * HEAD, kv_count * HEAD, 1).reshape(
        WIN + tok_rows, kv_count, HEAD
    )
    key_heads = jnp.repeat(key_sel, local_heads // kv_count, axis=1)
    value_heads = jnp.repeat(value_sel, local_heads // kv_count, axis=1)
    query_heads = queries.reshape(tok_rows, local_heads, HEAD)
    scores = jnp.einsum(
        "qhd,khd->hqk", query_heads, key_heads, preferred_element_type=jnp.float32
    ) * (1.0 / math.sqrt(HEAD))
    first_pos = slab_index * tok_rows
    q_pos = first_pos + jnp.arange(tok_rows, dtype=jnp.int32)
    k_pos = first_pos - WIN + jnp.arange(WIN + tok_rows, dtype=jnp.int32)
    allowed = (
        (k_pos[None, :] <= q_pos[:, None])
        & (k_pos[None, :] > q_pos[:, None] - WIN)
        & (k_pos[None, :] >= 0)
    )
    scores = jnp.where(allowed[None], scores, -1e30)
    row_top = jnp.maximum(jnp.max(scores, axis=-1), sink_logits[:, None])
    expo = jnp.exp(scores - row_top[..., None])
    denominator = jnp.sum(expo, axis=-1) + jnp.exp(sink_logits[:, None] - row_top)
    weights = (expo / denominator[..., None]).astype(jnp.bfloat16)
    context = jnp.einsum("hqk,khd->qhd", weights, value_heads, preferred_element_type=jnp.float32)
    context = context.astype(jnp.bfloat16).reshape(tok_rows, local_heads * HEAD)
    attn_part = jnp.dot(context, out_weight, preferred_element_type=jnp.float32)
    attn_piece = summed_rows(attn_part.astype(jnp.bfloat16), EXP, 0).astype(jnp.float32)
    piece_rows = attn_piece.shape[0]
    own_resid = lax.dynamic_slice_in_dim(residual, column * piece_rows, piece_rows, 0)
    mixed_share = (own_resid.astype(jnp.float32) + attn_piece).astype(jnp.bfloat16)
    normed_share = normalize(mixed_share, norm_gain)
    mixed, normed = side_by_side((mixed_share, normed_share), EXP, 0, 1)
    local_experts = gate_proj.shape[0]
    seq_count = lax.axis_size("seq")
    experts = local_experts * seq_count
    cap = 3 * tok_rows * TOP // (2 * experts)
    flat_ids = expert_ids.reshape(-1)
    onehot = (flat_ids[:, None] == jnp.arange(experts, dtype=jnp.int32)[None, :]).astype(jnp.int32)
    rank_ids = jnp.cumsum(onehot, axis=0) - 1
    slot_ids = jnp.sum(rank_ids * onehot, axis=1)
    targets = flat_ids * cap + slot_ids
    source = (
        jnp.full((experts * cap,), -1, jnp.int32)
        .at[targets]
        .set(jnp.arange(tok_rows * TOP, dtype=jnp.int32))
    )
    filled = source >= 0
    token_of = jnp.where(filled, source // TOP, 0)
    packed = jnp.where(filled[:, None], normed[token_of], jnp.zeros((), jnp.bfloat16))
    packed = packed.reshape(seq_count, local_experts, cap, packed.shape[1])
    slot_block = lax.all_to_all(packed, "seq", split_axis=0, concat_axis=0, tiled=True)
    gate_acc = jnp.einsum(
        "secd,edf->secf", slot_block, gate_proj, preferred_element_type=jnp.float32
    )
    up_acc = jnp.einsum("secd,edf->secf", slot_block, up_proj, preferred_element_type=jnp.float32)
    hidden = activate(gate_acc, up_acc)
    partial_out = jnp.einsum(
        "secf,efd->secd", hidden, down_proj, preferred_element_type=jnp.float32
    ).astype(jnp.bfloat16)
    returned = send_back(partial_out)
    flat_back = returned.reshape(experts * cap, returned.shape[3])
    picked = flat_back[targets].astype(jnp.float32).reshape(tok_rows, TOP, returned.shape[3])
    moe_part = jnp.sum(picked * route_gates[:, :, None], axis=1)
    moe_piece = summed_rows(moe_part.astype(jnp.bfloat16), EXP, 0).astype(jnp.float32)
    result_share = (mixed_share.astype(jnp.float32) + moe_piece).astype(jnp.bfloat16)
    return gather_directly(result_share, EXP, 0)


def solution(mesh):
    finer = Mesh(mesh.devices.reshape(mesh.shape["seq"], 8, 2), ("seq", "exp_0", "exp_1"))
    in_specs = (
        P("seq", EXP),
        P("seq", None),
        P("seq", None),
        P(EXP),
        P("seq", None),
        P(EXP, None),
        P(),
        P("seq", None),
        P("seq", None),
        P("seq", None, EXP),
        P("seq", None, EXP),
        P("seq", EXP, None),
    )
    out_specs = P("seq", None)
    return jax.shard_map(
        on_device, mesh=finer, in_specs=in_specs, out_specs=out_specs, check_vma=False
    )
```

profile of v0, /device:TPU:33, one launch (start us, length us, event | category | flops | bytes accessed | tf_op | source)
XLA Modules:
  0.0 598.7 jit_solution(17210189298612816052)
XLA Ops:
  6.5 1.1 slice.12
  7.6 3.7 collective-permute-start
  11.3 1.6 slice.13
  12.9 1.9 collective-permute-start.1
  18.7 1.1 copy-done.3
  20.2 1.9 convolution_convert_fusion.1
  22.2 1.8 convolution_convert_fusion
  24.0 39.7 %reduce-scatter.5.cloned.1.call-done = bf16[32,2880]{1,0:T(8,128)(2,1)} async-done(((bf16[256,2880]{1,0:T(8,128)(2,1)}), bf16[32,2880]{1,0:T(8,128)(2,1)}) %reduce-scatter.5.cloned.1.call-update) | async-done | bytes 184336 | tf_op jit(solution)/shard_map/reduce_scatter | solution.py:25
  63.8 2.2 constant_dynamic-slice_fusion
  66.1 1.4 copy.54
  67.4 19.8 %reduce-scatter.7.cloned.1.call-done = bf16[16,2880]{1,0:T(8,128)(2,1)} async-done(((bf16[32,2880]{1,0:T(8,128)(2,1)}), bf16[16,2880]{1,0:T(8,128)(2,1)}) %reduce-scatter.7.cloned.1.call-update) | async-done | bytes 92176 | tf_op jit(solution)/shard_map/reduce_scatter | solution.py:25
  90.3 31.1 %reduce-window.6 = s32[64,8,128]{2,1,0:T(8,128)S(1)} reduce-window(s32[64,8,128]{2,1,0:T(8,128)} %fusion.45, s32[]{:T(128)} %constant.33.clone.1), window={size=1x1x128 pad=0_0x0_0x127_0}, to_apply=%region_4.5 | reduce-window | flops 8323072 | bytes 524292 | tf_op jit(solution)/shard_map/reduce-window
  122.2 1.1 copy.43
  124.0 4.3 scatter_custom_fusion
  128.4 47.7 %all-gather.2.cloned.1.call-done = bf16[256,5760]{1,0:T(8,128)(2,1)} async-done(((bf16[16,5760]{1,0:T(8,128)(2,1)}), bf16[256,5760]{1,0:T(8,128)(2,1)}) %all-gather.2.cloned.1.call-update) | async-done | bytes 2949136 | tf_op jit(solution)/shard_map/all_gather | solution.py:32
  176.1 3.1 split.4
  179.2 18.6 %gather_fusion = bf16[1536,2880]{1,0:T(8,128)(2,1)} fusion(bf16[256,2880]{1,0:T(8,128)(2,1)} %split.4, s32[2048]{0:T(1024)S(1)} %pad_clamp_fusion), kind=kCustom, calls=%fused_computation | custom fusion | bytes 17700864 | tf_op jit(solution)/shard_map/gather | solution.py:142
  197.8 8.0 %broadcast_select_fusion = bf16[16,4,24,2880]{3,2,1,0:T(8,128)(2,1)} fusion(bf16[16,4,24,2880]{3,2,1,0:T(8,128)(2,1)} %bitcast.65, pred[16,4,24]{2,1,0:T(4,128)(4,1)S(1)} %broadcast_in_dim.37), kind=kLoop, calls=%fused_computation.5 | loop fusion | flops 4423680 | bytes 17696256 | tf_op jit(solution)/shard_map/jit(_where)/select_n | solution.py:142
  205.8 110.8 %all_to_all.15 = bf16[16,4,24,2880]{3,2,1,0:T(8,128)(2,1)S(1)} all-to-all(bf16[16,4,24,2880]{3,2,1,0:T(8,128)(2,1)} %broadcast_select_fusion), channel_id=1, replica_groups=mesh['seq'=16,'exp_0'=8,'exp_1'=2] {'seq'}, dimensions={0} | all-to-all | bytes 17694720 | tf_op jit(solution)/shard_map/all_to_all | solution.py:144
  316.6 3.5 copy-done.2
  320.1 3.7 fusion.18
  323.8 10.3 %convert_bitcast_fusion = bf16[16,4,24,2880]{3,2,0,1:T(8,128)(2,1)} fusion(bf16[4,128,2880]{1,2,0:T(8,128)(2,1)S(1)} %copy-done, f32[4,16,24,128]{3,2,1,0:T(8,128)} %fusion.18, bf16[4,2880,128]{2,1,0:T(8,128)(2,1)} %param.22, bf16[16,4,24,2880]{3,2,1,0:T(8,128)(2,1)} %copy-done.2), kind=kOutput, calls=%fused_computation.4 | convolution fusion | flops 2271117312 | bytes 24379392 | tf_op jit(solution)/shard_map/secf,efd->secd/dot_general | solution.py:150
  334.1 7.7 %copy.47 = bf16[16,4,24,2880]{3,2,1,0:T(8,128)(2,1)} copy(bf16[16,4,24,2880]{3,2,0,1:T(8,128)(2,1)} %convert_bitcast_fusion) | data formatting | bytes 17694720 | tf_op jit(solution)/shard_map/convert_element_type | solution.py:152
  341.8 5.3 all-to-all-start.1
  347.3 101.4 %all-to-all-done.1 = bf16[16,4,24,2880]{3,2,1,0:T(8,128)(2,1)} async-done(((bf16[16,4,24,2880]{3,2,1,0:T(8,128)(2,1)}), bf16[16,4,24,2880]{3,2,1,0:T(8,128)(2,1)}, u32[]{:S(2)}, u32[]{:S(2)}) %all-to-all-start.1) | async-done | bytes 8847392 | tf_op jit(solution)/shard_map/all_to_all | solution.py:65
  448.6 16.4 %gather_fusion.1 = bf16[1024,2880]{1,0:T(8,128)(2,1)} fusion(bf16[1536,2880]{1,0:T(8,128)(2,1)} %bitcast.17, s32[1024]{0:T(1024)S(1)} %broadcast_clamp_fusion), kind=kCustom, calls=%fused_computation.1 | custom fusion | bytes 11800576 | tf_op jit(solution)/shard_map/gather | solution.py:155
  465.0 11.7 %reshape.234 = f32[256,4,2880]{2,1,0:T(4,128)} reshape(bf16[1024,2880]{1,0:T(8,128)(2,1)} %gather_fusion.1) | data formatting | bytes 17694720 | tf_op jit(solution)/shard_map/convert_element_type | solution.py:155
  476.7 12.0 %multiply_reduce_fusion = bf16[256,2880]{1,0:T(8,128)(2,1)} fusion(f32[256,4,2880]{2,1,0:T(4,128)} %reshape.234, f32[256,4]{1,0:T(8,128)S(1)} %copy.48), kind=kLoop, calls=%fused_computation.3 | loop fusion | flops 5160960 | bytes 13275136 | tf_op jit(solution)/shard_map/reduce_sum | solution.py:156
  488.8 32.3 %reduce-scatter.9.cloned.1.call-done = bf16[32,2880]{1,0:T(8,128)(2,1)} async-done(((bf16[256,2880]{1,0:T(8,128)(2,1)}), bf16[32,2880]{1,0:T(8,128)(2,1)}) %reduce-scatter.9.cloned.1.call-update) | async-done | bytes 184336 | tf_op jit(solution)/shard_map/reduce_scatter | solution.py:25
  521.1 23.3 %reduce-scatter.11.cloned.1.call-done = bf16[16,2880]{1,0:T(8,128)(2,1)} async-done(((bf16[32,2880]{1,0:T(8,128)(2,1)}), bf16[16,2880]{1,0:T(8,128)(2,1)}) %reduce-scatter.11.cloned.1.call-update) | async-done | bytes 92176 | tf_op jit(solution)/shard_map/reduce_scatter | solution.py:25
  545.4 44.2 %all_to_all.16 = bf16[16,16,2880]{2,1,0:T(8,128)(2,1)} all-to-all(bf16[16,16,2880]{2,1,0:T(8,128)(2,1)S(1)} %broadcast_in_dim.63), channel_id=1, replica_groups=mesh['seq'=16,'exp_0'=8,'exp_1'=2] {'exp_0','exp_1'}, dimensions={0} | all-to-all | bytes 2949120 | tf_op jit(solution)/shard_map/all_to_all | solution.py:38
  589.6 2.5 copy.49
  (69 shorter events, 10.2 us)
Async XLA Ops:
  6.5 317.3 %copy-start = (bf16[4,128,2880]{1,2,0:T(8,128)(2,1)S(1)}, bf16[4,128,2880]{1,2,0:T(8,128)(2,1)}, u32[]{:S(2)}) copy-start(bf16[4,128,2880]{1,2,0:T(8,128)(2,1)} %param.23) | copy-start | bytes 8847364
  6.5 12.1 %copy-start.8 = (f32[4]{0:T(128)S(1)}, f32[4]{0:T(128)}, u32[]{:S(2)}) copy-start(f32[4]{0:T(128)} %param.15) | copy-start | bytes 52
  6.5 57.2 %reduce-scatter.5.cloned.1.call-start = ((), (), s32[]{:S(2)}) async-start(), calls=%async_computation.7 | async-start | bytes 1695744 | tf_op jit(solution)/shard_map/reduce_scatter | solution.py:25
  7.6 8.4 %collective-permute-start = (bf16[128,512]{1,0:T(8,128)(2,1)S(1)}, bf16[128,512]{1,0:T(8,128)(2,1)S(1)}, u32[]{:S(2)}, u32[]{:S(2)}) collective-permute-start(bf16[128,512]{1,0:T(8,128)(2,1)S(1)} %slice.12), channel_id=1, source_target_pairs={{0,16},{16,32},{32,48},{48,64},{64,80},{80,96},{96,112},{112,128},... | collective-permute-start | bytes 393224 | tf_op jit(solution)/shard_map/ppermute | solution.py:20
  12.9 4.2 collective-permute-start.1
  18.6 1.2 copy-start.3
  20.2 1.9 copy-start.4
  22.2 66.1 %copy-start.6 = (f32[2880]{0:T(1024)S(1)}, f32[2880]{0:T(1024)}, u32[]{:S(2)}) copy-start(f32[2880]{0:T(1024)} %param.18) | copy-start | bytes 34564
  23.9 65.2 %copy-start.5 = (s32[256,4]{0,1:T(4,128)S(1)}, s32[256,4]{0,1:T(4,128)}, u32[]{:S(2)}) copy-start(s32[256,4]{0,1:T(4,128)} %param.19) | copy-start | bytes 12292
  24.0 63.3 %reduce-scatter.7.cloned.1.call-start = ((), (), s32[]{:S(2)}) async-start(), calls=%async_computation.8 | async-start | bytes 282624 | tf_op jit(solution)/shard_map/reduce_scatter | solution.py:25
  63.8 112.4 %all-gather.2.cloned.1.call-start = ((), (), s32[]{:S(2)}) async-start(), calls=%async_computation.9 | async-start | bytes 3133440 | tf_op jit(solution)/shard_map/all_gather | solution.py:32
  205.8 114.3 %copy-start.9 = (bf16[4,2880,128]{2,1,0:T(8,128)(2,1)S(1)}, bf16[4,2880,128]{2,1,0:T(8,128)(2,1)}, u32[]{:S(2)}) copy-start(bf16[4,2880,128]{2,1,0:T(8,128)(2,1)} %param.21) | copy-start | bytes 8847364
  316.6 3.5 copy-start.2
  341.8 5.3 copy-start.7
  341.8 106.9 %all-to-all-start.1 = ((bf16[16,4,24,2880]{3,2,1,0:T(8,128)(2,1)}), bf16[16,4,24,2880]{3,2,1,0:T(8,128)(2,1)}, u32[]{:S(2)}, u32[]{:S(2)}) async-start(bf16[16,4,24,2880]{3,2,1,0:T(8,128)(2,1)} %copy.47), calls=%async_computation.3 | async-start | bytes 18087936 | tf_op jit(solution)/shard_map/all_to_all | solution.py:65
  347.0 174.0 %reduce-scatter.9.cloned.1.call-start = ((), (), s32[]{:S(2)}) async-start(), calls=%async_computation.10 | async-start | bytes 1695744 | tf_op jit(solution)/shard_map/reduce_scatter | solution.py:25
  488.8 55.6 %reduce-scatter.11.cloned.1.call-start = ((), (), s32[]{:S(2)}) async-start(), calls=%async_computation.11 | async-start | bytes 282624 | tf_op jit(solution)/shard_map/reduce_scatter | solution.py:25
  545.3 46.9 %copy-start.1 = (bf16[4,128,2880]{1,2,0:T(8,128)(2,1)S(1)}, bf16[4,128,2880]{1,2,0:T(8,128)(2,1)}, u32[]{:S(2)}) copy-start(bf16[4,128,2880]{1,2,0:T(8,128)(2,1)} %param.23) | copy-start | bytes 8847364
Sparse Core Ops, SparseCore 0:
  24.1 39.6 reduce-scatter.4
  66.2 20.9 reduce-scatter.6
  89.8 86.2 all-gather.1
  488.9 32.1 reduce-scatter.8
  523.4 20.9 reduce-scatter.10
where the time goes:
time: 604 us; the launch traced here: 599 us
  waiting for transfers between devices  265 us (44%)
  blocking collectives  155 us (26%)
  local copies, waits for them, and re-layouts  79.4 us (13%)
  other arithmetic  56.5 us (9%)
  matrix products  18.1 us (3%)
  between operations  13.5 us (2%)
  starting transfers between devices  11 us (2%)
    reduce_scatter x4, waiting for transfers between devices, summed_rows(): x = lax.psum_scatter(x, axis, scatter_dimension=dim, tiled=True)  115 us
    all_to_all x1, blocking collectives, on_device(): lax.all_to_all(packed, 'seq', split_axis=0, concat_axis=0, tiled=True)  111 us
    all_to_all x1, waiting for transfers between devices, send_back(): lax.all_to_all(partial_out, 'seq', split_axis=0, concat_axis=0, tiled=True)  101 us
    all_gather x1, waiting for transfers between devices, side_by_side(): out = lax.all_gather(both, axis, axis=dim, tiled=True)  47.7 us
    all_to_all x1, blocking collectives, from_everyone(): return lax.all_to_all(copies, axis, split_axis=0, concat_axis=0, tiled=True)  44.2 us
    another operation x2, other arithmetic  31.1 us
    gather x1, local copies, waits for them, and re-layouts, on_device(): normed[token_of]  18.6 us
    gather x1, local copies, waits for them, and re-layouts, on_device(): flat_back[targets].astype(jnp.float32)  16.4 us
  transfers between devices with their start and end apart: 8, of which 7 were waited for; matrix products, arithmetic and copies ran while one was open for 8% of the time, Pallas kernels for 0%

commit v1 on v0

v1 whole, which is shorter than its diff:
```python
import functools
import math

import jax
import jax.numpy as jnp
from jax import lax
from jax.experimental import pallas as pl
from jax.experimental.pallas import tpu as pltpu
from jax.sharding import PartitionSpec as P

HQ = 64
HK = 8
HEAD = 64
TOP = 4
WIN = 128
NS = 16
NE = 16
EXPERTS = 64
CAP = 24
SLOTS = 2 * CAP
QUAD = 4
MESH = pl.DeviceIdType.MESH
BF = jnp.bfloat16
F32 = jnp.float32


def passed_along(x, axis, by):
    count = lax.axis_size(axis)
    pairs = [(i, i + by) for i in range(count) if 0 <= i + by < count]
    return lax.ppermute(x, axis, pairs)


def attention(queries, key_rows, value_rows, sink_logits, out_weight):
    tok_rows = queries.shape[0]
    local_heads = queries.shape[1] // HEAD
    per_group = HQ // HK
    column = lax.axis_index("exp")
    slab_index = lax.axis_index("seq")
    kv_start = column * local_heads // per_group
    key_own = lax.dynamic_slice_in_dim(key_rows, kv_start * HEAD, HEAD, 1)
    value_own = lax.dynamic_slice_in_dim(value_rows, kv_start * HEAD, HEAD, 1)
    both = jnp.concatenate([key_own, value_own], 1)
    tail = passed_along(both[tok_rows - WIN :], "seq", 1)
    full = jnp.concatenate([tail, both], 0)
    key_full, value_full = full[:, :HEAD], full[:, HEAD:]
    query_heads = queries.reshape(tok_rows, local_heads, HEAD)
    scores = jnp.einsum("qhd,kd->hqk", query_heads, key_full, preferred_element_type=F32) * (
        1.0 / math.sqrt(HEAD)
    )
    first_pos = slab_index * tok_rows
    q_pos = first_pos + jnp.arange(tok_rows, dtype=jnp.int32)
    k_pos = first_pos - WIN + jnp.arange(WIN + tok_rows, dtype=jnp.int32)
    allowed = (
        (k_pos[None, :] <= q_pos[:, None])
        & (k_pos[None, :] > q_pos[:, None] - WIN)
        & (k_pos[None, :] >= 0)
    )
    scores = jnp.where(allowed[None], scores, -1e30)
    row_top = jnp.maximum(jnp.max(scores, axis=-1), sink_logits[:, None])
    expo = jnp.exp(scores - row_top[..., None])
    denominator = jnp.sum(expo, axis=-1) + jnp.exp(sink_logits[:, None] - row_top)
    weights = (expo / denominator[..., None]).astype(BF)
    context = jnp.einsum("hqk,kd->qhd", weights, value_full, preferred_element_type=F32)
    context = context.astype(BF).reshape(tok_rows, local_heads * HEAD)
    return jnp.dot(context, out_weight, preferred_element_type=F32).astype(BF)


def routing(expert_ids, route_gates, parity):
    rows = expert_ids.shape[0]
    half = EXPERTS // 2
    ids = jnp.arange(half, dtype=jnp.int32)
    mine = (ids // 2) * 4 + 2 * parity + ids % 2
    hits = expert_ids[:, :, None] == mine[None, None, :]
    named = jnp.sum(hits.astype(F32), axis=1)
    gate_of = jnp.sum(jnp.where(hits, route_gates[:, :, None], 0.0), axis=1)
    earlier = (jnp.arange(rows)[:, None] > jnp.arange(rows)[None, :]).astype(BF)
    count = jnp.dot(earlier, named.astype(BF), preferred_element_type=F32)
    slot_of = jnp.where(named > 0, count, -1.0).astype(BF)
    columns = jnp.arange(half * CAP, dtype=jnp.int32)
    spread = (columns[None, :] // CAP == ids[:, None]).astype(BF)
    slot_wide = jnp.dot(slot_of, spread, preferred_element_type=F32)
    taken = slot_wide == (columns % CAP).astype(F32)[None, :]
    gate_wide = jnp.dot(gate_of.astype(BF), spread, preferred_element_type=F32)
    combine = jnp.where(taken, gate_wide, 0.0).astype(BF)
    pick = taken.astype(BF).T
    quad_cols = QUAD * SLOTS
    combine = combine.reshape(rows, -1, quad_cols).transpose(1, 0, 2)
    return pick.reshape(-1, quad_cols, rows), combine


def layer_kernel(
    attn_ref,
    resid_ref,
    gain_ref,
    pick_ref,
    comb_ref,
    gate_ref,
    up_ref,
    down_ref,
    out_ref,
    parts,
    parts2,
    normed,
    mixed,
    packed,
    arrived,
    outgoing,
    returned,
    w_in,
    w_down,
    total,
    moe_part,
    w_local,
    w_send,
    w_recv,
    rs_send,
    rs_recv,
    ag_send,
    ag_recv,
    di_send,
    di_recv,
    re_send,
    re_recv,
    rs2_send,
    rs2_recv,
    ag2_send,
    ag2_recv,
    own_sem,
):
    s = lax.axis_index("seq")
    e = lax.axis_index("exp")
    parity = lax.rem(lax.div(e, 2), 2)
    partner = e + 2 - 4 * parity
    rows = normed.shape[0] // NE
    quad = lax.div(s, QUAD)
    hid = down_ref.shape[1]

    barrier = pltpu.get_barrier_semaphore()

    @pl.loop(1, NE)
    def _(d):
        pl.semaphore_signal(
            barrier, inc=1, device_id={"exp": lax.rem(e + d, NE)}, device_id_type=MESH
        )

    @pl.loop(1, NS)
    def _(d):
        pl.semaphore_signal(
            barrier, inc=1, device_id={"seq": lax.rem(s + d, NS)}, device_id_type=MESH
        )

    pl.semaphore_wait(barrier, NE + NS - 2)

    def rdma(src, dst, send, recv, **where):
        return pltpu.make_async_remote_copy(
            src_ref=src,
            dst_ref=dst,
            send_sem=send,
            recv_sem=recv,
            device_id=where,
            device_id_type=MESH,
        )

    def exp_block(i):
        return pl.ds(pl.multiple_of(i * rows, rows), rows)

    def rs_copy(src, dst, send, recv, to, frm):
        return rdma(src.at[exp_block(to)], dst.at[frm], send.at[to], recv.at[frm], exp=to)

    @pl.loop(1, NE)
    def _(d):
        to = lax.rem(e + d, NE)
        rs_copy(attn_ref, parts, rs_send, rs_recv, to, e).start()

    own = pltpu.make_async_copy(attn_ref.at[exp_block(e)], parts.at[e], own_sem.at[0])
    own.start()

    w_own, w_out = [], []
    for k in range(2):
        for j, ref in enumerate((gate_ref, up_ref)):
            col = k * 4 * hid + j * 2 * hid
            w_own.append((ref.at[2 * parity + k], w_in.at[:, pl.ds(col, hid)]))
            w_out.append((ref.at[2 - 2 * parity + k], w_in.at[:, pl.ds(col + hid, hid)]))
        row = k * 2 * hid
        w_own.append((down_ref.at[2 * parity + k], w_down.at[pl.ds(row, hid)]))
        w_out.append((down_ref.at[2 - 2 * parity + k], w_down.at[pl.ds(row + hid, hid)]))
    w_own = [pltpu.make_async_copy(a, b, w_local.at[i]) for i, (a, b) in enumerate(w_own)]
    w_out = [
        rdma(a, b, w_send.at[i], w_recv.at[i], exp=partner) for i, (a, b) in enumerate(w_out)
    ]
    for copy in w_own + w_out:
        copy.start()

    own.wait()

    @pl.loop(1, NE)
    def _(d):
        frm = lax.rem(e + d, NE)
        rs_copy(attn_ref, parts, rs_send, rs_recv, frm, frm).wait_recv()

    def summed(buf):
        acc = buf[0].astype(F32)
        for i in range(1, NE):
            acc += buf[i].astype(F32)
        return acc

    mixed_share = (resid_ref[...].astype(F32) + summed(parts)).astype(BF)
    mixed[...] = mixed_share
    wide = mixed_share.astype(F32)
    scale = lax.rsqrt(jnp.mean(wide * wide, axis=-1, keepdims=True) + 1e-05)
    normed[exp_block(e), :] = (wide * scale * gain_ref[...]).astype(BF)

    def ag_copy(buf, send, recv, to, frm):
        return rdma(buf.at[exp_block(frm)], buf.at[exp_block(frm)], send.at[to], recv.at[frm], exp=to)

    @pl.loop(1, NE)
    def _(d):
        to = lax.rem(e + d, NE)
        ag_copy(normed, ag_send, ag_recv, to, e).start()

    @pl.loop(1, NE)
    def _(d):
        frm = lax.rem(e + d, NE)
        ag_copy(normed, ag_send, ag_recv, frm, frm).wait_recv()

    def di_copy(to, frm):
        return rdma(packed.at[to], arrived.at[frm], di_send.at[to], di_recv.at[frm], seq=to)

    def self_copy():
        return pltpu.make_async_copy(packed.at[s], arrived.at[s], own_sem.at[1])

    for d in (2, 1, 3, 0):
        q = lax.rem(quad + d, NS // QUAD)
        block = jnp.dot(pick_ref[q], normed[...], preferred_element_type=F32).astype(BF)
        for j in range(QUAD):
            packed[q * QUAD + j] = block[j * SLOTS : (j + 1) * SLOTS]
        if d:
            for j in range(QUAD):
                di_copy(q * QUAD + j, s).start()
        else:
            for j in range(1, QUAD):
                di_copy(quad * QUAD + lax.rem(s + j, QUAD), s).start()
            self_copy().start()

    for copy in w_own:
        copy.wait()
    for copy in w_out:
        copy.wait_recv()

    def re_copy(to, frm):
        return rdma(outgoing.at[to], returned.at[frm], re_send.at[to], re_recv.at[frm], seq=to)

    def self_back():
        return pltpu.make_async_copy(outgoing.at[s], returned.at[s], own_sem.at[2])

    def activated(acc):
        gate = jnp.minimum(acc[:, : 2 * hid], 7.0)
        up = jnp.clip(acc[:, 2 * hid :], -7.0, 7.0)
        return (up + 1.0) * gate * jax.nn.sigmoid(1.702 * gate)

    for d in (0, 1, 3, 2):
        q = lax.rem(quad + d, NS // QUAD)
        if d:
            for j in range(QUAD):
                di_copy(q * QUAD + j, q * QUAD + j).wait_recv()
        else:
            for j in range(1, QUAD):
                frm = quad * QUAD + lax.rem(s + j, QUAD)
                di_copy(frm, frm).wait_recv()
            self_copy().wait()
        x = jnp.concatenate([arrived[q * QUAD + j] for j in range(QUAD)], 0)
        acc = jnp.dot(x, w_in[...], preferred_element_type=F32)
        slot = lax.rem(lax.broadcasted_iota(jnp.int32, (QUAD * SLOTS, 2 * hid), 0), SLOTS)
        first = jnp.where(slot < CAP, activated(acc[:, : 4 * hid]), 0.0)
        second = jnp.where(slot >= CAP, activated(acc[:, 4 * hid :]), 0.0)
        hidden = jnp.concatenate([first, second], 1).astype(BF)
        block = jnp.dot(hidden, w_down[...], preferred_element_type=F32).astype(BF)
        for j in range(QUAD):
            outgoing[q * QUAD + j] = block[j * SLOTS : (j + 1) * SLOTS]
        if d:
            for j in range(QUAD):
                re_copy(q * QUAD + j, s).start()
        else:
            for j in range(1, QUAD):
                re_copy(quad * QUAD + lax.rem(s + j, QUAD), s).start()
            self_back().start()

    for n, d in enumerate((0, 1, 3, 2)):
        q = lax.rem(quad + d, NS // QUAD)
        if d:
            for j in range(QUAD):
                re_copy(q * QUAD + j, q * QUAD + j).wait_recv()
        else:
            for j in range(1, QUAD):
                frm = quad * QUAD + lax.rem(s + j, QUAD)
                re_copy(frm, frm).wait_recv()
            self_back().wait()
        y = jnp.concatenate([returned[q * QUAD + j] for j in range(QUAD)], 0)
        add = jnp.dot(comb_ref[q], y, preferred_element_type=F32)
        if n == 0:
            total[...] = add
        elif n < 3:
            total[...] += add
        else:
            moe_part[...] = (total[...] + add).astype(BF)

    @pl.loop(1, NE)
    def _(d):
        to = lax.rem(e + d, NE)
        rs_copy(moe_part, parts2, rs2_send, rs2_recv, to, e).start()

    own2 = pltpu.make_async_copy(moe_part.at[exp_block(e)], parts2.at[e], own_sem.at[3])
    own2.start()
    own2.wait()

    @pl.loop(1, NE)
    def _(d):
        frm = lax.rem(e + d, NE)
        rs_copy(moe_part, parts2, rs2_send, rs2_recv, frm, frm).wait_recv()

    out_ref[exp_block(e), :] = (mixed[...].astype(F32) + summed(parts2)).astype(BF)

    @pl.loop(1, NE)
    def _(d):
        to = lax.rem(e + d, NE)
        ag_copy(out_ref, ag2_send, ag2_recv, to, e).start()

    @pl.loop(1, NE)
    def _(d):
        frm = lax.rem(e + d, NE)
        ag_copy(out_ref, ag2_send, ag2_recv, frm, frm).wait_recv()

    for copy in w_out:
        copy.wait_send()

    @pl.loop(1, NE)
    def _(d):
        to = lax.rem(e + d, NE)
        rs_copy(attn_ref, parts, rs_send, rs_recv, to, e).wait_send()
        ag_copy(normed, ag_send, ag_recv, to, e).wait_send()
        rs_copy(moe_part, parts2, rs2_send, rs2_recv, to, e).wait_send()
        ag_copy(out_ref, ag2_send, ag2_recv, to, e).wait_send()

    @pl.loop(1, NS)
    def _(d):
        to = lax.rem(s + d, NS)
        di_copy(to, s).wait_send()
        re_copy(to, s).wait_send()


def on_device(
    queries,
    key_rows,
    value_rows,
    sink_logits,
    residual,
    out_weight,
    norm_gain,
    expert_ids,
    route_gates,
    gate_proj,
    up_proj,
    down_proj,
):
    tok, width = residual.shape
    rows = tok // NE
    hid = down_proj.shape[1]
    column = lax.axis_index("exp")
    parity = (column // 2) % 2
    attn = attention(queries, key_rows, value_rows, sink_logits, out_weight)
    own_resid = lax.dynamic_slice_in_dim(residual, column * rows, rows, 0)
    pick, combine = routing(expert_ids, route_gates, parity)
    vmem = pl.BlockSpec(memory_space=pltpu.VMEM)
    hbm = pl.BlockSpec(memory_space=pl.ANY)
    dma = pltpu.SemaphoreType.DMA
    return pl.pallas_call(
        layer_kernel,
        out_shape=jax.ShapeDtypeStruct((tok, width), BF),
        in_specs=[vmem] * 5 + [hbm] * 3,
        out_specs=vmem,
        scratch_shapes=[
            pltpu.VMEM((NE, rows, width), BF),
            pltpu.VMEM((NE, rows, width), BF),
            pltpu.VMEM((tok, width), BF),
            pltpu.VMEM((rows, width), BF),
            pltpu.VMEM((NS, SLOTS, width), BF),
            pltpu.VMEM((NS, SLOTS, width), BF),
            pltpu.VMEM((NS, SLOTS, width), BF),
            pltpu.VMEM((NS, SLOTS, width), BF),
            pltpu.VMEM((width, 8 * hid), BF),
            pltpu.VMEM((4 * hid, width), BF),
            pltpu.VMEM((tok, width), F32),
            pltpu.VMEM((tok, width), BF),
            dma((6,)),
            dma((6,)),
            dma((6,)),
        ]
        + [dma((NE,))] * 12
        + [dma((4,))],
        compiler_params=pltpu.CompilerParams(
            collective_id=0, has_side_effects=True, vmem_limit_bytes=62 * 1024 * 1024
        ),
    )(attn, own_resid, norm_gain.reshape(1, width), pick, combine, gate_proj, up_proj, down_proj)


def solution(mesh):
    in_specs = (
        P("seq", "exp"),
        P("seq", None),
        P("seq", None),
        P("exp"),
        P("seq", None),
        P("exp", None),
        P(),
        P("seq", None),
        P("seq", None),
        P("seq", None, "exp"),
        P("seq", None, "exp"),
        P("seq", "exp", None),
    )
    return jax.shard_map(
        on_device, mesh=mesh, in_specs=in_specs, out_specs=P("seq", None), check_vma=False
    )
```

time: 604 us -> 380 us (0.63)
  the two profiles are of different devices: /device:TPU:33 before, /device:TPU:1 now
where the time goes in v1:
time: 380 us; the launch traced here: 379 us
  Pallas kernels  354 us (93%)
  local copies, waits for them, and re-layouts  15.2 us (4%)
  starting transfers between devices  4.49 us (1%)
    pallas_call x1, Pallas kernels, on_device(): pl.pallas_call(layer_kernel, out_shape=jax.ShapeDtypeStruct((tok, width),...  354 us
  transfers between devices with their start and end apart: 1, of which 0 were waited for; matrix products, arithmetic and copies ran while one was open for 3% of the time, Pallas kernels for 0%

profile of v1, /device:TPU:1, one launch (start us, length us, event | category | flops | bytes accessed | tf_op | source)
XLA Modules:
  0.0 379.5 jit_solution(15576487744881628541)
XLA Ops:
  0.0 1.1 constant_dynamic-slice_fusion.1
  1.1 0.1 copy.61
  1.2 0.1 copy.60
  1.3 0.0 copy-start.2
  1.3 0.6 pad_maximum_fusion
  1.9 4.5 %collective-permute-start = (bf16[128,128]{0,1:T(8,128)(2,1)}, bf16[128,128]{0,1:T(8,128)(2,1)}, u32[]{:S(2)}, u32[]{:S(2)}) collective-permute-start(bf16[128,128]{0,1:T(8,128)(2,1)} %pad_maximum_fusion), channel_id=1, source_target_pairs={{0,16},{16,32},{32,48},{48,64},{64,80},{80,96},{96,112},{112,128},... | collective-permute-start | bytes 98312 | tf_op jit(solution)/shard_map/ppermute | solution.py:30
  6.5 0.8 fusion.4
  7.3 0.5 convolution_compare_fusion
  7.8 0.0 copy-start.5
  7.9 0.0 copy-start.4
  7.9 0.1 convert_bitcast_fusion
  8.0 0.3 fusion.1
  8.3 1.4 constant_dynamic-slice_fusion
  9.7 0.8 and_and_fusion
  10.5 0.6 reshape.211.gain_ref
  11.1 0.1 copy.50
  11.2 0.2 copy.54
  11.3 1.0 copy.55
  12.3 0.9 copy.53
  13.3 0.9 copy.62.resid_ref
  14.2 4.6 %copy.57.down_ref = bf16[4,128,2880]{2,1,0:T(8,128)(2,1)} copy(bf16[4,128,2880]{1,2,0:T(8,128)(2,1)} %param.23) | data formatting | bytes 5898240 | tf_op args[11]
  18.8 0.0 collective-permute-done
  18.8 0.8 maximum_maximum_fusion
  19.6 0.4 fusion.26
  20.0 0.1 broadcast_maximum_fusion
  20.0 0.2 fusion
  20.3 0.1 exponential_add_fusion
  20.4 0.4 convolution_convert_fusion.1
  20.8 0.5 convolution_convert_fusion
  21.3 1.7 copy.56.attn_ref
  23.0 353.9 %shard_map.118 = bf16[256,2880]{1,0:T(8,128)(2,1)} custom-call(bf16[256,2880]{1,0:T(8,128)(2,1)} %copy.56.attn_ref, bf16[16,2880]{1,0:T(8,128)(2,1)} %copy.62.resid_ref, f32[1,2880]{1,0:T(1,128)} %reshape.211.gain_ref, bf16[4,192,256]{2,1,0:T(8,128)(2,1)} %bitcast.24, bf16[4,256,192]{2,1,0:T(8,128)(2,1)} %bitcast.23, bf16[4,2880,128]{2,1,0:T(8,128)(2,1)} %gate_ref.1, ...), custom_call_target="tpu_custom_call" | custom-call | tf_op jit(solution)/shard_map/pallas_call | solution.py:376
  376.9 2.5 copy.58
  (16 shorter events, 0.1 us)
Async XLA Ops:
  0.0 20.8 %copy-start = (bf16[256,2880]{0,1:T(8,128)(2,1)S(1)}, bf16[256,2880]{0,1:T(8,128)(2,1)}, u32[]{:S(2)}) copy-start(bf16[256,2880]{0,1:T(8,128)(2,1)} %param.17) | copy-start | bytes 4423684
  1.3 6.0 %copy-start.2 = (bf16[256,64]{0,1:T(8,128)(2,1)}, bf16[256,64]{0,1:T(8,128)(2,1)S(1)}, u32[]{:S(2)}) copy-start(bf16[256,64]{0,1:T(8,128)(2,1)S(1)} %copy.60) | copy-start | bytes 98308
  1.9 16.8 %collective-permute-start = (bf16[128,128]{0,1:T(8,128)(2,1)}, bf16[128,128]{0,1:T(8,128)(2,1)}, u32[]{:S(2)}, u32[]{:S(2)}) collective-permute-start(bf16[128,128]{0,1:T(8,128)(2,1)} %pad_maximum_fusion), channel_id=1, source_target_pairs={{0,16},{16,32},{32,48},{48,64},{64,80},{80,96},{96,112},{112,128},... | collective-permute-start | bytes 98312 | tf_op jit(solution)/shard_map/ppermute | solution.py:30
  7.8 2.6 copy-start.5
  7.9 3.2 copy-start.4
  14.1 4.6 %copy-start.3 = (bf16[256,64]{0,1:T(8,128)(2,1)S(1)}, bf16[256,64]{0,1:T(8,128)(2,1)}, u32[]{:S(2)}) copy-start(bf16[256,64]{0,1:T(8,128)(2,1)} %copy-done.2) | copy-start | bytes 98308
  14.2 5.4 %copy-start.1 = (pred[256,384]{0,1:T(8,128)(4,1)S(1)}, pred[256,384]{0,1:T(8,128)(4,1)}, u32[]{:S(2)}) copy-start(pred[256,384]{0,1:T(8,128)(4,1)} %and_and_fusion) | copy-start | bytes 294916
  18.8 1.2 copy-start.6

commit v2 on v1

v2 whole, which is shorter than its diff:
```python
import functools
import math

import jax
import jax.numpy as jnp
from jax import lax
from jax.experimental import pallas as pl
from jax.experimental.pallas import tpu as pltpu
from jax.sharding import PartitionSpec as P

HQ = 64
HK = 8
HEAD = 64
TOP = 4
WIN = 128
NS = 16
NE = 16
EXPERTS = 64
CAP = 24
SLOTS = 2 * CAP
QUAD = 4
NZ = 8
CUTS = (0, 768, 1536, 2304, 2880)
CHUNKS = tuple((a, b - a) for a, b in zip(CUTS, CUTS[1:]))
NC = len(CHUNKS)
NC_BOTH = 2
MESH = pl.DeviceIdType.MESH
BF = jnp.bfloat16
F32 = jnp.float32


def passed_along(x, axis, by):
    count = lax.axis_size(axis)
    pairs = [(i, i + by) for i in range(count) if 0 <= i + by < count]
    return lax.ppermute(x, axis, pairs)


def attention(queries, key_rows, value_rows, sink_logits, out_weight):
    tok_rows = queries.shape[0]
    local_heads = queries.shape[1] // HEAD
    per_group = HQ // HK
    column = lax.axis_index("exp")
    slab_index = lax.axis_index("seq")
    kv_start = column * local_heads // per_group
    key_own = lax.dynamic_slice_in_dim(key_rows, kv_start * HEAD, HEAD, 1)
    value_own = lax.dynamic_slice_in_dim(value_rows, kv_start * HEAD, HEAD, 1)
    both = jnp.concatenate([key_own, value_own], 1)
    tail = passed_along(both[tok_rows - WIN :], "seq", 1)
    full = jnp.concatenate([tail, both], 0)
    key_full, value_full = full[:, :HEAD], full[:, HEAD:]
    query_heads = queries.reshape(tok_rows, local_heads, HEAD)
    scores = jnp.einsum("qhd,kd->hqk", query_heads, key_full, preferred_element_type=F32) * (
        1.0 / math.sqrt(HEAD)
    )
    first_pos = slab_index * tok_rows
    q_pos = first_pos + jnp.arange(tok_rows, dtype=jnp.int32)
    k_pos = first_pos - WIN + jnp.arange(WIN + tok_rows, dtype=jnp.int32)
    allowed = (
        (k_pos[None, :] <= q_pos[:, None])
        & (k_pos[None, :] > q_pos[:, None] - WIN)
        & (k_pos[None, :] >= 0)
    )
    scores = jnp.where(allowed[None], scores, -1e30)
    row_top = jnp.maximum(jnp.max(scores, axis=-1), sink_logits[:, None])
    expo = jnp.exp(scores - row_top[..., None])
    denominator = jnp.sum(expo, axis=-1) + jnp.exp(sink_logits[:, None] - row_top)
    weights = (expo / denominator[..., None]).astype(BF)
    context = jnp.einsum("hqk,kd->qhd", weights, value_full, preferred_element_type=F32)
    context = context.astype(BF).reshape(tok_rows, local_heads * HEAD)
    return jnp.dot(context, out_weight, preferred_element_type=F32).astype(BF)


def routing(expert_ids, route_gates, parity):
    rows = expert_ids.shape[0]
    half = EXPERTS // 2
    ids = jnp.arange(half, dtype=jnp.int32)
    mine = (ids // 2) * 4 + 2 * parity + ids % 2
    hits = expert_ids[:, :, None] == mine[None, None, :]
    named = jnp.sum(hits.astype(F32), axis=1)
    gate_of = jnp.sum(jnp.where(hits, route_gates[:, :, None], 0.0), axis=1)
    earlier = (jnp.arange(rows)[:, None] > jnp.arange(rows)[None, :]).astype(BF)
    count = jnp.dot(earlier, named.astype(BF), preferred_element_type=F32)
    slot_of = jnp.where(named > 0, count, -1.0).astype(BF)
    columns = jnp.arange(half * CAP, dtype=jnp.int32)
    spread = (columns[None, :] // CAP == ids[:, None]).astype(BF)
    slot_wide = jnp.dot(slot_of, spread, preferred_element_type=F32)
    taken = slot_wide == (columns % CAP).astype(F32)[None, :]
    gate_wide = jnp.dot(gate_of.astype(BF), spread, preferred_element_type=F32)
    combine = jnp.where(taken, gate_wide, 0.0).astype(BF)
    pick = taken.astype(BF).T
    quad_cols = QUAD * SLOTS
    combine = combine.reshape(rows, -1, quad_cols).transpose(1, 0, 2)
    return pick.reshape(-1, quad_cols, rows), combine


def layer_kernel(
    attn_ref,
    resid_ref,
    gain_ref,
    pick_ref,
    comb_ref,
    gate_ref,
    up_ref,
    down_ref,
    out_ref,
    xin,
    zsrc,
    zin,
    zin2,
    pair,
    pair_in,
    normed,
    mixed,
    packed,
    arrived,
    outgoing,
    returned,
    w_in,
    w_down,
    acc,
    hidden,
    moe_part,
    result,
    w_local,
    w_send,
    w_recv,
    rx_send,
    rx_recv,
    rz_send,
    rz_recv,
    gx_send,
    gx_recv,
    gz_send,
    gz_recv,
    mx_send,
    mx_recv,
    di_send,
    di_recv,
    re_send,
    re_recv,
    own_sem,
):
    s = lax.axis_index("seq")
    e = lax.axis_index("exp")
    z = lax.div(e, 2)
    xh = lax.rem(e, 2)
    parity = lax.rem(z, 2)
    mate = e + 2 - 4 * parity
    across = e + 1 - 2 * xh
    rows = mixed.shape[1]
    quad = lax.div(s, QUAD)
    hid = gate_ref.shape[2]
    tok = NE * rows

    barrier = pltpu.get_barrier_semaphore()

    @pl.loop(1, NE)
    def _(d):
        pl.semaphore_signal(
            barrier, inc=1, device_id={"exp": lax.rem(e + d, NE)}, device_id_type=MESH
        )

    @pl.loop(1, NS)
    def _(d):
        pl.semaphore_signal(
            barrier, inc=1, device_id={"seq": lax.rem(s + d, NS)}, device_id_type=MESH
        )

    pl.semaphore_wait(barrier, NE + NS - 2)

    def rdma(src, dst, send, recv, **where):
        return pltpu.make_async_remote_copy(
            src_ref=src,
            dst_ref=dst,
            send_sem=send,
            recv_sem=recv,
            device_id=where,
            device_id_type=MESH,
        )

    def cols(c):
        return pl.ds(*CHUNKS[c])

    def other(d):
        return lax.rem(z + d, NZ)

    def rx(c):
        return rdma(
            attn_ref.at[:, 1 - xh, :, cols(c)],
            xin.at[:, :, cols(c)],
            rx_send.at[0, c],
            rx_recv.at[0, c],
            exp=across,
        )

    def rz(c, to, frm):
        return rdma(
            zsrc.at[to, :, cols(c)],
            zin.at[frm, :, cols(c)],
            rz_send.at[0, c],
            rz_recv.at[0, c],
            exp=2 * to + xh,
        )

    def rz_all(c):
        part = zin.at[pl.ds(0, NZ - 1), :, cols(c)]
        return rdma(part, part, rz_send.at[0, c], rz_recv.at[0, c], exp=across)

    def rx_done_rz_start(c):
        rx(c).wait_recv()
        both = attn_ref[:, xh, :, cols(c)].astype(F32) + xin[:, :, cols(c)].astype(F32)
        zsrc[:, :, cols(c)] = both.astype(BF)

        @pl.loop(1, NZ)
        def _(d):
            rz(c, other(NZ - d), z).start()

    def rz_sum(c):
        rz_all(c).wait_recv()
        sum_ = zsrc[z, :, cols(c)].astype(F32)
        for d in range(1, NZ):
            sum_ += zin[other(d), :, cols(c)].astype(F32)
        return sum_

    def ez(c, to, frm):
        return rdma(
            moe_part.at[to, :, :, cols(c)],
            zin2.at[frm, :, :, cols(c)],
            rz_send.at[1, c],
            rz_recv.at[1, c],
            exp=2 * to + xh,
        )

    def ez_all(c):
        part = zin2.at[pl.ds(0, NZ - 1), :, :, cols(c)]
        return rdma(part, part, rz_send.at[1, c], rz_recv.at[1, c], exp=across)

    def ez_start(c):
        @pl.loop(1, NZ)
        def _(d):
            ez(c, other(NZ - d), z).start()

    def ex(c):
        return rdma(
            pair.at[:, :, cols(c)],
            pair_in.at[:, :, cols(c)],
            rx_send.at[1, c],
            rx_recv.at[1, c],
            exp=across,
        )

    def ez_done_ex_start(c):
        ez_all(c).wait_recv()
        sum_ = moe_part[z, :, :, cols(c)].astype(F32)
        for d in range(1, NZ):
            sum_ += zin2[other(d), :, :, cols(c)].astype(F32)
        pair[:, :, cols(c)] = sum_.astype(BF)
        ex(c).start()

    def mixed_across(half):
        return rdma(mixed.at[half], mixed.at[half], mx_send.at[0], mx_recv.at[0], exp=across)

    def gz(n, c, to, frm):
        if n == 1 and c < NC_BOTH:
            block = result.at[frm, :, :, cols(c)]
        else:
            block = (normed, result)[n].at[frm, xh, :, cols(c)]
        return rdma(block, block, gz_send.at[n, c], gz_recv.at[n, c], exp=2 * to + xh)

    def gz_start(n, c):
        @pl.loop(1, NZ)
        def _(d):
            gz(n, c, other(NZ - d), z).start()

    def gz_all(n, c):
        if n == 1 and c < NC_BOTH:
            part = result.at[pl.ds(0, NZ - 1), :, :, cols(c)]
        else:
            part = (normed, result)[n].at[pl.ds(0, NZ - 1), xh, :, cols(c)]
        return rdma(part, part, gz_send.at[n, c], gz_recv.at[n, c], exp=across)

    def gz_wait(n, c):
        gz_all(n, c).wait_recv()

    def gx(n, c, half):
        buf = (normed, result)[n]
        block = buf.at[:, half, :, cols(c)]
        return rdma(block, block, gx_send.at[n, c], gx_recv.at[n, c], exp=across)

    def gz_done_gx_start(n, c):
        gz_wait(n, c)
        gx(n, c, xh).start()

    def weight_pairs(c):
        keep, give = [], []
        for ref in (gate_ref, up_ref, down_ref):
            for k in range(2):
                at = (0, 2 * hid, 0)[len(keep) // 2] + k * (2 if ref is down_ref else 4) * hid
                buf = w_down if ref is down_ref else w_in
                keep.append((ref.at[2 * parity + k, cols(c)], buf.at[cols(c), pl.ds(at, hid)]))
                give.append(
                    (ref.at[2 - 2 * parity + k, cols(c)], buf.at[cols(c), pl.ds(at + hid, hid)])
                )
        keep = [pltpu.make_async_copy(a, b, w_local.at[c, i]) for i, (a, b) in enumerate(keep)]
        give = [
            rdma(a, b, w_send.at[c, i], w_recv.at[c, i], exp=mate) for i, (a, b) in enumerate(give)
        ]
        return keep, give

    weights = [weight_pairs(c) for c in range(NC)]

    queue = [copy for c in range(NC) for copy in weights[c][1][:4]]
    queue += [copy for c in range(NC) for copy in weights[c][1][4:]]

    def give(count):
        for copy in queue[:count]:
            copy.start()
        del queue[:count]

    for c in range(NC):
        rx(c).start()
    give(2)
    for c in range(NC):
        for copy in weights[c][0]:
            copy.start()
    for c in range(NC):
        rx_done_rz_start(c)
    pick_own = (
        lax.broadcasted_iota(jnp.int32, (rows, tok), 1)
        == e * rows + lax.broadcasted_iota(jnp.int32, (rows, tok), 0)
    ).astype(BF)
    square = jnp.zeros((rows, 1), F32)
    for c in range(NC):
        own = lax.dot_general(
            pick_own,
            resid_ref[cols(c), :],
            (((1,), (1,)), ((), ())),
            preferred_element_type=F32,
        )
        mine = (own + rz_sum(c)).astype(BF)
        mixed[xh, :, cols(c)] = mine
        wide = mine.astype(F32)
        square += jnp.sum(wide * wide, axis=-1, keepdims=True)
    scale = lax.rsqrt(square / mixed.shape[2] + 1e-05)
    for c in range(NC):
        wide = mixed[xh, :, cols(c)].astype(F32)
        normed[z, xh, :, cols(c)] = (wide * scale * gain_ref[:, cols(c)]).astype(BF)
        gz_start(0, c)
    mixed_across(xh).start()
    give(len(queue))

    def di(c, to, frm, d=0):
        return rdma(
            packed.at[to, :, cols(c)],
            arrived.at[frm, :, cols(c)],
            di_send.at[c],
            di_recv.at[c, d],
            seq=to,
        )

    def di_own(c):
        return pltpu.make_async_copy(
            packed.at[s, :, cols(c)], arrived.at[s, :, cols(c)], own_sem.at[0, c]
        )

    def re(c, to, frm, d=0):
        return rdma(
            outgoing.at[to, :, cols(c)],
            returned.at[frm, :, cols(c)],
            re_send.at[c],
            re_recv.at[c, d],
            seq=to,
        )

    def re_own(c):
        return pltpu.make_async_copy(
            outgoing.at[s, :, cols(c)], returned.at[s, :, cols(c)], own_sem.at[1, c]
        )

    def peers(d):
        if d:
            q = lax.rem(quad + d, NS // QUAD)
            return [q * QUAD + j for j in range(QUAD)]
        return [quad * QUAD + lax.rem(s + j, QUAD) for j in range(1, QUAD)]

    def put(buf, q, c, block):
        for j in range(QUAD):
            buf[q * QUAD + j, :, cols(c)] = block[j * SLOTS : (j + 1) * SLOTS]

    def start(copy, own, d, c):
        for to in peers(d):
            copy(c, to, s, (NS // QUAD - d) % (NS // QUAD)).start()
        if d == 0:
            own(c).start()

    def group(copy, c, d, count):
        buf = arrived if copy is di else returned
        part = buf.at[pl.ds(0, count), :, cols(c)]
        send, recv = (di_send, di_recv) if copy is di else (re_send, re_recv)
        return rdma(part, part, send.at[c], recv.at[c, d], exp=across)

    def wait(copy, own, d, c):
        group(copy, c, d, QUAD if d else QUAD - 1).wait_recv()
        if d == 0:
            own(c).wait()

    def pack(c):
        gx(0, c, 1 - xh).wait_recv()
        full = normed[:, :, :, cols(c)].reshape(tok, CHUNKS[c][1])
        for d in (2, 1, 3, 0):
            q = lax.rem(quad + d, NS // QUAD)
            put(packed, q, c, jnp.dot(pick_ref[q], full, preferred_element_type=F32).astype(BF))
            start(di, di_own, d, c)

    for c in range(NC):
        gz_done_gx_start(0, c)
    for c in range(NC):
        pack(c)

    for c in range(NC):
        for copy in weights[c][0]:
            copy.wait()
        for copy in weights[c][1][:4]:
            copy.wait_recv()
        for d in (0, 1, 3, 2):
            q = lax.rem(quad + d, NS // QUAD)
            wait(di, di_own, d, c)
            x = jnp.concatenate([arrived[q * QUAD + j, :, cols(c)] for j in range(QUAD)], 0)
            add = jnp.dot(x, w_in[cols(c), :], preferred_element_type=F32)
            if c:
                acc[q] += add
            else:
                acc[q] = add

    def activated(block):
        gate = jnp.minimum(block[:, : 2 * hid], 7.0)
        up = jnp.clip(block[:, 2 * hid :], -7.0, 7.0)
        return (up + 1.0) * gate * jax.nn.sigmoid(1.702 * gate)

    slot = lax.rem(lax.broadcasted_iota(jnp.int32, (QUAD * SLOTS, 2 * hid), 0), SLOTS)
    for q in range(NS // QUAD):
        first = jnp.where(slot < CAP, activated(acc[q, :, : 4 * hid]), 0.0)
        second = jnp.where(slot >= CAP, activated(acc[q, :, 4 * hid :]), 0.0)
        hidden[q] = jnp.concatenate([first, second], 1).astype(BF)

    def give_back(c):
        for copy in weights[c][1][4:]:
            copy.wait_recv()
        for d in (2, 1, 3, 0):
            q = lax.rem(quad + d, NS // QUAD)
            block = lax.dot_general(
                hidden[q],
                w_down[cols(c), :],
                (((1,), (1,)), ((), ())),
                preferred_element_type=F32,
            )
            put(outgoing, q, c, block.astype(BF))
            start(re, re_own, d, c)

    def combine(c):
        sum_ = None
        for d in (0, 1, 3, 2):
            q = lax.rem(quad + d, NS // QUAD)
            wait(re, re_own, d, c)
            y = jnp.concatenate([returned[q * QUAD + j, :, cols(c)] for j in range(QUAD)], 0)
            add = jnp.dot(comb_ref[q], y, preferred_element_type=F32)
            sum_ = add if sum_ is None else sum_ + add
        moe_part[:, :, :, cols(c)] = sum_.astype(BF).reshape(NZ, 2, rows, CHUNKS[c][1])
        ez_start(c)

    def finish_rows(c):
        ex(c).wait_recv()
        mine = slice(None) if c < NC_BOTH else xh
        both = pair[mine, :, cols(c)].astype(F32) + pair_in[mine, :, cols(c)].astype(F32)
        done = mixed[mine, :, cols(c)].astype(F32) + both
        result[z, mine, :, cols(c)] = done.astype(BF)
        gz_start(1, c)

    def write_out(c):
        if c < NC_BOTH:
            gz_wait(1, c)
        else:
            gx(1, c, 1 - xh).wait_recv()
        out_ref[cols(c), :] = result[:, :, :, cols(c)].reshape(tok, CHUNKS[c][1]).T

    give_back(0)
    give_back(1)
    mixed_across(1 - xh).wait_recv()
    for c in range(NC):
        combine(c)
        if c:
            finish_rows(c - 1)
        ez_done_ex_start(c)
        if c + 2 < NC:
            give_back(c + 2)
    finish_rows(NC - 1)
    for c in range(NC):
        if c >= NC_BOTH:
            gz_done_gx_start(1, c)
        else:
            write_out(c)
    for c in range(NC_BOTH, NC):
        write_out(c)

    mixed_across(xh).wait_send()
    for c in range(NC):
        for copy in weights[c][1]:
            copy.wait_send()
        rx(c).wait_send()
        ex(c).wait_send()
        gx(0, c, xh).wait_send()
        if c >= NC_BOTH:
            gx(1, c, xh).wait_send()

        rz_all(c).wait_send()
        ez_all(c).wait_send()
        gz_all(0, c).wait_send()
        gz_all(1, c).wait_send()
        group(di, c, 0, NS - 1).wait_send()
        group(re, c, 0, NS - 1).wait_send()


def on_device(
    queries,
    key_rows,
    value_rows,
    sink_logits,
    residual,
    out_weight,
    norm_gain,
    expert_ids,
    route_gates,
    gate_proj,
    up_proj,
    down_proj,
):
    tok, width = residual.shape
    rows = tok // NE
    hid = down_proj.shape[1]
    column = lax.axis_index("exp")
    parity = (column // 2) % 2
    attn = attention(queries, key_rows, value_rows, sink_logits, out_weight)
    pick, combine = routing(expert_ids, route_gates, parity)
    vmem = pl.BlockSpec(memory_space=pltpu.VMEM)
    hbm = pl.BlockSpec(memory_space=pl.ANY)
    dma = pltpu.SemaphoreType.DMA
    sums = [pltpu.VMEM((NZ, rows, width), BF)] * 3
    slots = pltpu.VMEM((NS, SLOTS, width), BF)
    whole = pltpu.VMEM((NZ, 2, rows, width), BF)
    both = pltpu.VMEM((2, rows, width), BF)
    out = pl.pallas_call(
        layer_kernel,
        out_shape=jax.ShapeDtypeStruct((width, tok), BF),
        in_specs=[vmem] * 5 + [hbm] * 3,
        out_specs=vmem,
        scratch_shapes=sums
        + [whole, both, both]
        + [
            whole,
            both,
            slots,
            slots,
            slots,
            slots,
            pltpu.VMEM((width, 8 * hid), BF),
            pltpu.VMEM((width, 4 * hid), BF),
            pltpu.VMEM((NS // QUAD, QUAD * SLOTS, 8 * hid), F32),
            pltpu.VMEM((NS // QUAD, QUAD * SLOTS, 4 * hid), BF),
            whole,
            whole,
        ]
        + [dma((NC, 6))] * 3
        + [dma((2, NC))] * 8
        + [dma((1,))] * 2
        + [dma((NC,)), dma((NC, NS // QUAD))] * 2
        + [dma((2, NC))],
        compiler_params=pltpu.CompilerParams(
            collective_id=0, has_side_effects=True, vmem_limit_bytes=62 * 1024 * 1024
        ),
    )(
        attn.reshape(NZ, 2, rows, width),
        residual.T,
        norm_gain.reshape(1, width),
        pick,
        combine,
        gate_proj,
        up_proj,
        down_proj.transpose(0, 2, 1),
    )
    return out.T


def solution(mesh):
    in_specs = (
        P("seq", "exp"),
        P("seq", None),
        P("seq", None),
        P("exp"),
        P("seq", None),
        P("exp", None),
        P(),
        P("seq", None),
        P("seq", None),
        P("seq", None, "exp"),
        P("seq", None, "exp"),
        P("seq", "exp", None),
    )
    return jax.shard_map(
        on_device, mesh=mesh, in_specs=in_specs, out_specs=P("seq", None), check_vma=False
    )
```

time: 380 us -> 235 us (0.62)
  the two profiles are of different devices: /device:TPU:1 before, /device:TPU:33 now
where the time goes in v2:
time: 235 us; the launch traced here: 232 us
  Pallas kernels  216 us (92%)
  local copies, waits for them, and re-layouts  8.59 us (4%)
  starting transfers between devices  3.81 us (2%)
    pallas_call x1, Pallas kernels, on_device(): pl.pallas_call(layer_kernel, out_shape=jax.ShapeDtypeStruct((width, tok),...  216 us
  transfers between devices with their start and end apart: 1, of which 0 were waited for; matrix products, arithmetic and copies ran while one was open for 2% of the time, Pallas kernels for 0%

profile of v2, /device:TPU:33, one launch (start us, length us, event | category | flops | bytes accessed | tf_op | source)
XLA Modules:
  0.0 232.1 jit_solution(18309465040704183291)
XLA Ops:
  0.0 0.0 copy-start
  0.0 1.1 constant_dynamic-slice_fusion
  1.1 0.1 copy.41
  1.2 0.1 copy.40
  1.3 0.0 copy-start.2
  1.3 0.0 copy-start.1
  1.3 3.8 %collective-permute-start = (bf16[128,128]{0,1:T(8,128)(2,1)S(1)}, bf16[128,128]{0,1:T(8,128)(2,1)S(1)}, u32[]{:S(2)}, u32[]{:S(2)}) collective-permute-start(bf16[128,128]{0,1:T(8,128)(2,1)S(1)} %pad_maximum_fusion), channel_id=1, source_target_pairs={{0,16},{16,32},{32,48},{48,64},{64,80},{80,96},{96,112},{112,128},... | collective-permute-start | bytes 98312 | tf_op jit(solution)/shard_map/ppermute | solution.py:35
  5.3 0.8 fusion.4
  6.1 0.5 convolution_compare_fusion
  6.6 0.1 convert_bitcast_fusion
  6.7 0.3 fusion.1
  7.0 0.2 and_and_fusion
  7.1 0.0 copy-done.2
  7.2 0.6 reshape.215.gain_ref
  7.8 0.0 copy-done.1
  7.8 0.1 copy.33
  7.9 0.2 copy.37
  8.0 1.0 copy.38
  9.0 0.0 copy-start.3
  9.1 0.9 copy.36
  10.0 0.0 collective-permute-done
  10.0 0.4 fusion.26
  10.4 0.0 copy-done.3
  10.4 0.1 broadcast_maximum_fusion
  10.5 0.2 fusion
  10.7 0.1 exponential_add_fusion
  10.8 0.4 convolution_convert_fusion.1
  11.2 0.0 copy-done
  11.2 0.5 convolution_convert_fusion
  11.8 1.9 copy.35
  13.7 215.9 %shard_map.118 = bf16[2880,256]{1,0:T(8,128)(2,1)} custom-call(bf16[8,2,16,2880]{3,2,1,0:T(8,128)(2,1)} %bitcast.27, bf16[2880,256]{1,0:T(8,128)(2,1)} %bitcast.33, f32[1,2880]{1,0:T(1,128)} %reshape.215.gain_ref, bf16[4,192,256]{2,1,0:T(8,128)(2,1)} %bitcast.31, bf16[4,256,192]{2,1,0:T(8,128)(2,1)} %bitcast.30, bf16[4,2880,128]{2,1,0:T(8,128)(2,1)} %gate_ref.1, ...), custom_call_target="tpu_custom_call" | custom-call | tf_op jit(solution)/shard_map/pallas_call | solution.py:551
  229.6 2.6 %copy.45 = bf16[256,2880]{0,1:T(8,128)(2,1)} copy(bf16[256,2880]{0,1:T(8,128)(2,1)} %bitcast.28) | data formatting | bytes 2949120
  (7 shorter events, 0.1 us)
Async XLA Ops:
  0.0 11.2 %copy-start = (bf16[256,2880]{0,1:T(8,128)(2,1)S(1)}, bf16[256,2880]{0,1:T(8,128)(2,1)}, u32[]{:S(2)}) copy-start(bf16[256,2880]{0,1:T(8,128)(2,1)} %param.17) | copy-start | bytes 4423684
  1.3 5.8 %copy-start.2 = (f32[2880]{0:T(1024)S(1)}, f32[2880]{0:T(1024)}, u32[]{:S(2)}) copy-start(f32[2880]{0:T(1024)} %param.18) | copy-start | bytes 34564
  1.3 6.4 %copy-start.1 = (bf16[256,256]{1,0:T(8,128)(2,1)S(1)}, bf16[256,256]{1,0:T(8,128)(2,1)}, u32[]{:S(2)}) copy-start(bf16[256,256]{1,0:T(8,128)(2,1)} %param.12) | copy-start | bytes 393220
  1.3 8.7 %collective-permute-start = (bf16[128,128]{0,1:T(8,128)(2,1)S(1)}, bf16[128,128]{0,1:T(8,128)(2,1)S(1)}, u32[]{:S(2)}, u32[]{:S(2)}) collective-permute-start(bf16[128,128]{0,1:T(8,128)(2,1)S(1)} %pad_maximum_fusion), channel_id=1, source_target_pairs={{0,16},{16,32},{32,48},{48,64},{64,80},{80,96},{96,112},{112,128},... | collective-permute-start | bytes 98312 | tf_op jit(solution)/shard_map/ppermute | solution.py:35
  9.0 1.4 copy-start.3

commit v3 on v2

--- a/solution.py
+++ b/solution.py
@@ -29,80 +29,27 @@
 F32 = jnp.float32
 
 
-def passed_along(x, axis, by):
-    count = lax.axis_size(axis)
-    pairs = [(i, i + by) for i in range(count) if 0 <= i + by < count]
-    return lax.ppermute(x, axis, pairs)
-
-
-def attention(queries, key_rows, value_rows, sink_logits, out_weight):
-    tok_rows = queries.shape[0]
-    local_heads = queries.shape[1] // HEAD
-    per_group = HQ // HK
-    column = lax.axis_index("exp")
-    slab_index = lax.axis_index("seq")
-    kv_start = column * local_heads // per_group
-    key_own = lax.dynamic_slice_in_dim(key_rows, kv_start * HEAD, HEAD, 1)
-    value_own = lax.dynamic_slice_in_dim(value_rows, kv_start * HEAD, HEAD, 1)
-    both = jnp.concatenate([key_own, value_own], 1)
-    tail = passed_along(both[tok_rows - WIN :], "seq", 1)
-    full = jnp.concatenate([tail, both], 0)
-    key_full, value_full = full[:, :HEAD], full[:, HEAD:]
-    query_heads = queries.reshape(tok_rows, local_heads, HEAD)
-    scores = jnp.einsum("qhd,kd->hqk", query_heads, key_full, preferred_element_type=F32) * (
-        1.0 / math.sqrt(HEAD)
-    )
-    first_pos = slab_index * tok_rows
-    q_pos = first_pos + jnp.arange(tok_rows, dtype=jnp.int32)
-    k_pos = first_pos - WIN + jnp.arange(WIN + tok_rows, dtype=jnp.int32)
-    allowed = (
-        (k_pos[None, :] <= q_pos[:, None])
-        & (k_pos[None, :] > q_pos[:, None] - WIN)
-        & (k_pos[None, :] >= 0)
-    )
-    scores = jnp.where(allowed[None], scores, -1e30)
-    row_top = jnp.maximum(jnp.max(scores, axis=-1), sink_logits[:, None])
-    expo = jnp.exp(scores - row_top[..., None])
-    denominator = jnp.sum(expo, axis=-1) + jnp.exp(sink_logits[:, None] - row_top)
-    weights = (expo / denominator[..., None]).astype(BF)
-    context = jnp.einsum("hqk,kd->qhd", weights, value_full, preferred_element_type=F32)
-    context = context.astype(BF).reshape(tok_rows, local_heads * HEAD)
-    return jnp.dot(context, out_weight, preferred_element_type=F32).astype(BF)
-
-
-def routing(expert_ids, route_gates, parity):
-    rows = expert_ids.shape[0]
-    half = EXPERTS // 2
-    ids = jnp.arange(half, dtype=jnp.int32)
-    mine = (ids // 2) * 4 + 2 * parity + ids % 2
-    hits = expert_ids[:, :, None] == mine[None, None, :]
-    named = jnp.sum(hits.astype(F32), axis=1)
-    gate_of = jnp.sum(jnp.where(hits, route_gates[:, :, None], 0.0), axis=1)
-    earlier = (jnp.arange(rows)[:, None] > jnp.arange(rows)[None, :]).astype(BF)
-    count = jnp.dot(earlier, named.astype(BF), preferred_element_type=F32)
-    slot_of = jnp.where(named > 0, count, -1.0).astype(BF)
-    columns = jnp.arange(half * CAP, dtype=jnp.int32)
-    spread = (columns[None, :] // CAP == ids[:, None]).astype(BF)
-    slot_wide = jnp.dot(slot_of, spread, preferred_element_type=F32)
-    taken = slot_wide == (columns % CAP).astype(F32)[None, :]
-    gate_wide = jnp.dot(gate_of.astype(BF), spread, preferred_element_type=F32)
-    combine = jnp.where(taken, gate_wide, 0.0).astype(BF)
-    pick = taken.astype(BF).T
-    quad_cols = QUAD * SLOTS
-    combine = combine.reshape(rows, -1, quad_cols).transpose(1, 0, 2)
-    return pick.reshape(-1, quad_cols, rows), combine
-
-
 def layer_kernel(
-    attn_ref,
-    resid_ref,
+    query_ref,
+    sink_ref,
     gain_ref,
-    pick_ref,
-    comb_ref,
+    ids_ref,
+    gates_ref,
+    key_ref,
+    value_ref,
+    proj_ref,
+    skip_ref,
     gate_ref,
     up_ref,
     down_ref,
     out_ref,
+    keys,
+    values,
+    proj,
+    resid,
+    pick,
+    comb,
+    attn,
     xin,
     zsrc,
     zin,
@@ -139,19 +86,37 @@
     re_send,
     re_recv,
     own_sem,
+    load_sem,
+    halo_send,
+    halo_recv,
 ):
     s = lax.axis_index("seq")
     e = lax.axis_index("exp")
     z = lax.div(e, 2)
     xh = lax.rem(e, 2)
-    parity = lax.rem(z, 2)
-    mate = e + 2 - 4 * parity
+    parity = lax.rem(z + s, 2)
+    mate = 2 * lax.rem(z + 1 + (NZ - 2) * parity, NZ) + xh
     across = e + 1 - 2 * xh
     rows = mixed.shape[1]
     quad = lax.div(s, QUAD)
     hid = gate_ref.shape[2]
     tok = NE * rows
 
+    lanes = pl.ds(pl.multiple_of(lax.div(e, 4) * 2 * HEAD, 2 * HEAD), 2 * HEAD)
+    loads = [
+        pltpu.make_async_copy(src, dst, load_sem.at[i])
+        for i, (src, dst) in enumerate(
+            (
+                (key_ref.at[:, lanes], keys.at[pl.ds(WIN, tok)]),
+                (value_ref.at[:, lanes], values.at[pl.ds(WIN, tok)]),
+                (proj_ref, proj),
+                (skip_ref, resid),
+            )
+        )
+    ]
+    for copy in loads:
+        copy.start()
+
     barrier = pltpu.get_barrier_semaphore()
 
     @pl.loop(1, NE)
@@ -166,6 +131,38 @@
             barrier, inc=1, device_id={"seq": lax.rem(s + d, NS)}, device_id_type=MESH
         )
 
+    def head_of(buf, at):
+        both = buf[pl.ds(at, 2 * WIN), :]
+        return jnp.where(lax.rem(lax.div(e, 2), 2) == 1, both[:, HEAD:], both[:, :HEAD])
+
+    def context(half):
+        heads = query_ref.shape[1] // HEAD
+        at = half * WIN
+        query = jnp.concatenate(
+            [query_ref[at : at + WIN, h * HEAD : (h + 1) * HEAD] for h in range(heads)], 0
+        )
+        scores = lax.dot_general(
+            query, head_of(keys, at), (((1,), (1,)), ((), ())), preferred_element_type=F32
+        ) * (1.0 / math.sqrt(HEAD))
+        row = lax.rem(lax.broadcasted_iota(jnp.int32, scores.shape, 0), WIN)
+        col = lax.broadcasted_iota(jnp.int32, scores.shape, 1)
+        allowed = (col > row) & (col <= row + WIN)
+        if half == 0:
+            allowed = allowed & ((col >= WIN) | (s > 0))
+        scores = jnp.where(allowed, scores, -1e30)
+        sink = jnp.concatenate(
+            [jnp.broadcast_to(sink_ref[:, h : h + 1], (WIN, 1)) for h in range(heads)], 0
+        )
+        top = jnp.maximum(jnp.max(scores, axis=-1, keepdims=True), sink)
+        expo = jnp.exp(scores - top)
+        total = jnp.sum(expo, axis=-1, keepdims=True) + jnp.exp(sink - top)
+        weights = (expo / total).astype(BF)
+        out = jnp.dot(weights, head_of(values, at), preferred_element_type=F32).astype(BF)
+        return jnp.concatenate([out[h * WIN : (h + 1) * WIN] for h in range(heads)], 1)
+
+    loads[0].wait()
+    loads[1].wait()
+    second = context(1)
     pl.semaphore_wait(barrier, NE + NS - 2)
 
     def rdma(src, dst, send, recv, **where):
@@ -186,7 +183,7 @@
 
     def rx(c):
         return rdma(
-            attn_ref.at[:, 1 - xh, :, cols(c)],
+            attn.at[:, 1 - xh, :, cols(c)],
             xin.at[:, :, cols(c)],
             rx_send.at[0, c],
             rx_recv.at[0, c],
@@ -208,7 +205,7 @@
 
     def rx_done_rz_start(c):
         rx(c).wait_recv()
-        both = attn_ref[:, xh, :, cols(c)].astype(F32) + xin[:, :, cols(c)].astype(F32)
+        both = attn[:, xh, :, cols(c)].astype(F32) + xin[:, :, cols(c)].astype(F32)
         zsrc[:, :, cols(c)] = both.astype(BF)
 
         @pl.loop(1, NZ)
@@ -317,12 +314,64 @@
             copy.start()
         del queue[:count]
 
-    for c in range(NC):
-        rx(c).start()
-    give(2)
+    halo = [
+        rdma(
+            ref.at[pl.ds(tok - WIN, WIN), lanes],
+            buf.at[pl.ds(0, WIN)],
+            halo_send.at[i],
+            halo_recv.at[i],
+            seq=lax.rem(s + 1, NS),
+        )
+        for i, (ref, buf) in enumerate(((key_ref, keys), (value_ref, values)))
+    ]
+    for copy in halo:
+        copy.start()
+    give(4)
     for c in range(NC):
         for copy in weights[c][0]:
             copy.start()
+    loads[2].wait()
+    for copy in halo:
+        copy.wait_recv()
+    mixed_heads = jnp.concatenate([context(0), second], 0)
+    for c in range(NC):
+        part = lax.dot_general(
+            mixed_heads, proj[cols(c), :], (((1,), (1,)), ((), ())), preferred_element_type=F32
+        )
+        attn[:, :, :, cols(c)] = part.astype(BF).reshape(NZ, 2, rows, CHUNKS[c][1])
+        rx(c).start()
+
+    half = EXPERTS // 2
+    index = lax.broadcasted_iota(jnp.int32, (half, tok), 0)
+    group_of = lax.div(index, 2)
+    mine = 4 * group_of + 2 * lax.rem(group_of + z, 2) + lax.rem(index, 2)
+    named = jnp.zeros((half, tok), F32)
+    gate_of = jnp.zeros((half, tok), F32)
+    for k in range(TOP):
+        hit = ids_ref[k : k + 1, :] == mine
+        named += jnp.where(hit, 1.0, 0.0)
+        gate_of += jnp.where(hit, gates_ref[k : k + 1, :], 0.0)
+    earlier = lax.broadcasted_iota(jnp.int32, (tok, tok), 0) < lax.broadcasted_iota(
+        jnp.int32, (tok, tok), 1
+    )
+    count = jnp.dot(
+        named.astype(BF), jnp.where(earlier, 1.0, 0.0).astype(BF), preferred_element_type=F32
+    )
+    slot_of = jnp.where(named > 0.0, count, -1.0).astype(BF)
+    gate_of = gate_of.astype(BF)
+    for q in range(NS // QUAD):
+        shape = (QUAD * SLOTS, half)
+        place = lax.div(lax.broadcasted_iota(jnp.int32, shape, 0), CAP) + q * 2 * QUAD
+        spread = jnp.where(place == lax.broadcasted_iota(jnp.int32, shape, 1), 1.0, 0.0)
+        spread = spread.astype(BF)
+        wide = jnp.dot(spread, slot_of, preferred_element_type=F32)
+        number = lax.rem(lax.broadcasted_iota(jnp.int32, (QUAD * SLOTS, tok), 0), CAP)
+        taken = wide == number.astype(F32)
+        gate_wide = jnp.dot(spread, gate_of, preferred_element_type=F32)
+        pick[q] = jnp.where(taken, 1.0, 0.0).astype(BF)
+        comb[q] = jnp.where(taken, gate_wide, 0.0).T.astype(BF)
+    loads[3].wait()
+
     for c in range(NC):
         rx_done_rz_start(c)
     pick_own = (
@@ -333,7 +382,7 @@
     for c in range(NC):
         own = lax.dot_general(
             pick_own,
-            resid_ref[cols(c), :],
+            resid[cols(c), :],
             (((1,), (1,)), ((), ())),
             preferred_element_type=F32,
         )
@@ -409,7 +458,7 @@
         full = normed[:, :, :, cols(c)].reshape(tok, CHUNKS[c][1])
         for d in (2, 1, 3, 0):
             q = lax.rem(quad + d, NS // QUAD)
-            put(packed, q, c, jnp.dot(pick_ref[q], full, preferred_element_type=F32).astype(BF))
+            put(packed, q, c, jnp.dot(pick[q], full, preferred_element_type=F32).astype(BF))
             start(di, di_own, d, c)
 
     for c in range(NC):
@@ -463,7 +512,7 @@
             q = lax.rem(quad + d, NS // QUAD)
             wait(re, re_own, d, c)
             y = jnp.concatenate([returned[q * QUAD + j, :, cols(c)] for j in range(QUAD)], 0)
-            add = jnp.dot(comb_ref[q], y, preferred_element_type=F32)
+            add = jnp.dot(comb[q], y, preferred_element_type=F32)
             sum_ = add if sum_ is None else sum_ + add
         moe_part[:, :, :, cols(c)] = sum_.astype(BF).reshape(NZ, 2, rows, CHUNKS[c][1])
         ez_start(c)
@@ -503,6 +552,8 @@
         write_out(c)
 
     mixed_across(xh).wait_send()
+    for copy in halo:
+        copy.wait_send()
     for c in range(NC):
         for copy in weights[c][1]:
             copy.wait_send()
@@ -537,10 +588,6 @@
     tok, width = residual.shape
     rows = tok // NE
     hid = down_proj.shape[1]
-    column = lax.axis_index("exp")
-    parity = (column // 2) % 2
-    attn = attention(queries, key_rows, value_rows, sink_logits, out_weight)
-    pick, combine = routing(expert_ids, route_gates, parity)
     vmem = pl.BlockSpec(memory_space=pltpu.VMEM)
     hbm = pl.BlockSpec(memory_space=pl.ANY)
     dma = pltpu.SemaphoreType.DMA
@@ -551,9 +598,18 @@
     out = pl.pallas_call(
         layer_kernel,
         out_shape=jax.ShapeDtypeStruct((width, tok), BF),
-        in_specs=[vmem] * 5 + [hbm] * 3,
+        in_specs=[vmem] * 5 + [hbm] * 7,
         out_specs=vmem,
-        scratch_shapes=sums
+        scratch_shapes=[
+            pltpu.VMEM((WIN + tok, 2 * HEAD), BF),
+            pltpu.VMEM((WIN + tok, 2 * HEAD), BF),
+            pltpu.VMEM((width, queries.shape[1]), BF),
+            pltpu.VMEM((width, tok), BF),
+            pltpu.VMEM((NS // QUAD, QUAD * SLOTS, tok), BF),
+            pltpu.VMEM((NS // QUAD, tok, QUAD * SLOTS), BF),
+            whole,
+        ]
+        + sums
         + [whole, both, both]
         + [
             whole,
@@ -573,16 +629,20 @@
         + [dma((2, NC))] * 8
         + [dma((1,))] * 2
         + [dma((NC,)), dma((NC, NS // QUAD))] * 2
-        + [dma((2, NC))],
+        + [dma((2, NC)), dma((4,)), dma((2,)), dma((2,))],
         compiler_params=pltpu.CompilerParams(
             collective_id=0, has_side_effects=True, vmem_limit_bytes=62 * 1024 * 1024
         ),
     )(
-        attn.reshape(NZ, 2, rows, width),
+        queries,
+        sink_logits.reshape(1, -1),
+        norm_gain.reshape(1, width),
+        expert_ids.T,
+        route_gates.T,
+        key_rows,
+        value_rows,
+        out_weight.T,
         residual.T,
-        norm_gain.reshape(1, width),
-        pick,
-        combine,
         gate_proj,
         up_proj,
         down_proj.transpose(0, 2, 1),

time: 235 us -> 213 us (0.906); the launches traced: 232 us -> 213 us
  Pallas kernels: 216 us -> 209 us
  local copies, waits for them, and re-layouts: 8.59 us -> 3.89 us
  starting transfers between devices: 3.81 us -> 0 us
    pallas_call x1, Pallas kernels: 216 us -> 209 us  [on_device(): pl.pallas_call(layer_kernel, out_shape=jax.ShapeDtypeStruct((width, tok),...]
    ppermute x1 -> x0, starting transfers between devices: 3.81 us -> none  [passed_along(): return lax.ppermute(x, axis, pairs)]
  transfers between devices with their start and end apart: 1 -> 0, of which waited for: 0 -> 0; matrix products, arithmetic and copies ran while one was open for 2% -> 0% of each run, Pallas kernels for 0% -> 0%
where the time goes in v3:
time: 213 us
  Pallas kernels  209 us (98%)
  local copies, waits for them, and re-layouts  3.89 us (2%)
    pallas_call x1, Pallas kernels, on_device(): pl.pallas_call(layer_kernel, out_shape=jax.ShapeDtypeStruct((width, tok),...  209 us

profile of v3, /device:TPU:33, one launch (start us, length us, event | category | flops | bytes accessed | tf_op | source)
XLA Modules:
  0.0 213.1 jit_solution(10861235198353212753)
XLA Ops:
  0.0 1.3 reshape.7.gain_ref
  1.3 209.2 %shard_map.118 = bf16[2880,256]{1,0:T(8,128)(2,1)} custom-call(bf16[256,256]{1,0:T(8,128)(2,1)} %query_ref.1, f32[1,4]{1,0:T(1,128)} %bitcast.13, f32[1,2880]{1,0:T(1,128)} %reshape.7.gain_ref, s32[4,256]{1,0:T(4,128)} %bitcast.11, f32[4,256]{1,0:T(4,128)} %bitcast.12, bf16[256,512]{1,0:T(8,128)(2,1)} %key_ref.1, bf16[256,512]{1,0:T(8,128)(2,1)} %value_ref.1, ...), custom_call_target="tpu_custom_call" | custom-call | tf_op jit(solution)/shard_map/pallas_call | solution.py:598
  210.6 2.6 %copy.14 = bf16[256,2880]{0,1:T(8,128)(2,1)} copy(bf16[256,2880]{0,1:T(8,128)(2,1)} %bitcast.7) | data formatting | bytes 2949120

commit v4 on v3

--- a/solution.py
+++ b/solution.py
@@ -20,10 +20,13 @@
 SLOTS = 2 * CAP
 QUAD = 4
 NZ = 8
-CUTS = (0, 768, 1536, 2304, 2880)
-CHUNKS = tuple((a, b - a) for a, b in zip(CUTS, CUTS[1:]))
-NC = len(CHUNKS)
-NC_BOTH = 2
+CUTS = (0, 640, 1280, 1920, 2432, 2880)
+LATE_CUTS = (0, 384, 1152, 1920, 2560, 2880)
+CHUNKS = tuple(
+    tuple((a, b - a) for a, b in zip(cuts, cuts[1:])) for cuts in (CUTS, LATE_CUTS)
+)
+NC = len(CHUNKS[0])
+NC_BOTH = 1
 MESH = pl.DeviceIdType.MESH
 BF = jnp.bfloat16
 F32 = jnp.float32
@@ -175,8 +178,8 @@
             device_id_type=MESH,
         )
 
-    def cols(c):
-        return pl.ds(*CHUNKS[c])
+    def cols(c, late=0):
+        return pl.ds(*CHUNKS[late][c])
 
     def other(d):
         return lax.rem(z + d, NZ)
@@ -221,15 +224,15 @@
 
     def ez(c, to, frm):
         return rdma(
-            moe_part.at[to, :, :, cols(c)],
-            zin2.at[frm, :, :, cols(c)],
+            moe_part.at[to, :, :, cols(c, 1)],
+            zin2.at[frm, :, :, cols(c, 1)],
             rz_send.at[1, c],
             rz_recv.at[1, c],
             exp=2 * to + xh,
         )
 
     def ez_all(c):
-        part = zin2.at[pl.ds(0, NZ - 1), :, :, cols(c)]
+        part = zin2.at[pl.ds(0, NZ - 1), :, :, cols(c, 1)]
         return rdma(part, part, rz_send.at[1, c], rz_recv.at[1, c], exp=across)
 
     def ez_start(c):
@@ -239,8 +242,8 @@
 
     def ex(c):
         return rdma(
-            pair.at[:, :, cols(c)],
-            pair_in.at[:, :, cols(c)],
+            pair.at[:, :, cols(c, 1)],
+            pair_in.at[:, :, cols(c, 1)],
             rx_send.at[1, c],
             rx_recv.at[1, c],
             exp=across,
@@ -248,20 +251,22 @@
 
     def ez_done_ex_start(c):
         ez_all(c).wait_recv()
-        sum_ = moe_part[z, :, :, cols(c)].astype(F32)
+        sum_ = moe_part[z, :, :, cols(c, 1)].astype(F32)
         for d in range(1, NZ):
-            sum_ += zin2[other(d), :, :, cols(c)].astype(F32)
-        pair[:, :, cols(c)] = sum_.astype(BF)
+            sum_ += zin2[other(d), :, :, cols(c, 1)].astype(F32)
+        pair[:, :, cols(c, 1)] = sum_.astype(BF)
         ex(c).start()
 
     def mixed_across(half):
         return rdma(mixed.at[half], mixed.at[half], mx_send.at[0], mx_recv.at[0], exp=across)
 
     def gz(n, c, to, frm):
-        if n == 1 and c < NC_BOTH:
-            block = result.at[frm, :, :, cols(c)]
+        if n == 0:
+            block = normed.at[frm, :, :, cols(c)]
+        elif c < NC_BOTH:
+            block = result.at[frm, :, :, cols(c, 1)]
         else:
-            block = (normed, result)[n].at[frm, xh, :, cols(c)]
+            block = result.at[frm, xh, :, cols(c, 1)]
         return rdma(block, block, gz_send.at[n, c], gz_recv.at[n, c], exp=2 * to + xh)
 
     def gz_start(n, c):
@@ -270,23 +275,20 @@
             gz(n, c, other(NZ - d), z).start()
 
     def gz_all(n, c):
-        if n == 1 and c < NC_BOTH:
-            part = result.at[pl.ds(0, NZ - 1), :, :, cols(c)]
+        if n == 0:
+            part = normed.at[pl.ds(0, NZ - 1), :, :, cols(c)]
+        elif c < NC_BOTH:
+            part = result.at[pl.ds(0, NZ - 1), :, :, cols(c, 1)]
         else:
-            part = (normed, result)[n].at[pl.ds(0, NZ - 1), xh, :, cols(c)]
+            part = result.at[pl.ds(0, NZ - 1), xh, :, cols(c, 1)]
         return rdma(part, part, gz_send.at[n, c], gz_recv.at[n, c], exp=across)
 
-    def gz_wait(n, c):
-        gz_all(n, c).wait_recv()
-
     def gx(n, c, half):
-        buf = (normed, result)[n]
-        block = buf.at[:, half, :, cols(c)]
+        if n == 0:
+            block = normed.at[z, half, :, cols(c)]
+        else:
+            block = result.at[:, half, :, cols(c, 1)]
         return rdma(block, block, gx_send.at[n, c], gx_recv.at[n, c], exp=across)
-
-    def gz_done_gx_start(n, c):
-        gz_wait(n, c)
-        gx(n, c, xh).start()
 
     def weight_pairs(c):
         keep, give = [], []
@@ -294,10 +296,9 @@
             for k in range(2):
                 at = (0, 2 * hid, 0)[len(keep) // 2] + k * (2 if ref is down_ref else 4) * hid
                 buf = w_down if ref is down_ref else w_in
-                keep.append((ref.at[2 * parity + k, cols(c)], buf.at[cols(c), pl.ds(at, hid)]))
-                give.append(
-                    (ref.at[2 - 2 * parity + k, cols(c)], buf.at[cols(c), pl.ds(at + hid, hid)])
-                )
+                span = cols(c, int(ref is down_ref))
+                keep.append((ref.at[2 * parity + k, span], buf.at[span, pl.ds(at, hid)]))
+                give.append((ref.at[2 - 2 * parity + k, span], buf.at[span, pl.ds(at + hid, hid)]))
         keep = [pltpu.make_async_copy(a, b, w_local.at[c, i]) for i, (a, b) in enumerate(keep)]
         give = [
             rdma(a, b, w_send.at[c, i], w_recv.at[c, i], exp=mate) for i, (a, b) in enumerate(give)
@@ -338,7 +339,7 @@
         part = lax.dot_general(
             mixed_heads, proj[cols(c), :], (((1,), (1,)), ((), ())), preferred_element_type=F32
         )
-        attn[:, :, :, cols(c)] = part.astype(BF).reshape(NZ, 2, rows, CHUNKS[c][1])
+        attn[:, :, :, cols(c)] = part.astype(BF).reshape(NZ, 2, rows, CHUNKS[0][c][1])
         rx(c).start()
 
     half = EXPERTS // 2
@@ -393,9 +394,12 @@
     scale = lax.rsqrt(square / mixed.shape[2] + 1e-05)
     for c in range(NC):
         wide = mixed[xh, :, cols(c)].astype(F32)
-        normed[z, xh, :, cols(c)] = (wide * scale * gain_ref[:, cols(c)]).astype(BF)
+        normed[z, xh, :, cols(c)] = (wide * scale * gain_ref[cols(c)].reshape(1, -1)).astype(BF)
+        gx(0, c, xh).start()
+    mixed_across(xh).start()
+    for c in range(NC):
+        gx(0, c, 1 - xh).wait_recv()
         gz_start(0, c)
-    mixed_across(xh).start()
     give(len(queue))
 
     def di(c, to, frm, d=0):
@@ -414,8 +418,8 @@
 
     def re(c, to, frm, d=0):
         return rdma(
-            outgoing.at[to, :, cols(c)],
-            returned.at[frm, :, cols(c)],
+            outgoing.at[to, :, cols(c, 1)],
+            returned.at[frm, :, cols(c, 1)],
             re_send.at[c],
             re_recv.at[c, d],
             seq=to,
@@ -423,7 +427,7 @@
 
     def re_own(c):
         return pltpu.make_async_copy(
-            outgoing.at[s, :, cols(c)], returned.at[s, :, cols(c)], own_sem.at[1, c]
+            outgoing.at[s, :, cols(c, 1)], returned.at[s, :, cols(c, 1)], own_sem.at[1, c]
         )
 
     def peers(d):
@@ -433,8 +437,9 @@
         return [quad * QUAD + lax.rem(s + j, QUAD) for j in range(1, QUAD)]
 
     def put(buf, q, c, block):
+        span = cols(c, int(buf is outgoing))
         for j in range(QUAD):
-            buf[q * QUAD + j, :, cols(c)] = block[j * SLOTS : (j + 1) * SLOTS]
+            buf[q * QUAD + j, :, span] = block[j * SLOTS : (j + 1) * SLOTS]
 
     def start(copy, own, d, c):
         for to in peers(d):
@@ -444,7 +449,7 @@
 
     def group(copy, c, d, count):
         buf = arrived if copy is di else returned
-        part = buf.at[pl.ds(0, count), :, cols(c)]
+        part = buf.at[pl.ds(0, count), :, cols(c, int(copy is re))]
         send, recv = (di_send, di_recv) if copy is di else (re_send, re_recv)
         return rdma(part, part, send.at[c], recv.at[c, d], exp=across)
 
@@ -454,98 +459,114 @@
             own(c).wait()
 
     def pack(c):
-        gx(0, c, 1 - xh).wait_recv()
-        full = normed[:, :, :, cols(c)].reshape(tok, CHUNKS[c][1])
+        gz_all(0, c).wait_recv()
+        full = normed[:, :, :, cols(c)].reshape(tok, CHUNKS[0][c][1])
         for d in (2, 1, 3, 0):
             q = lax.rem(quad + d, NS // QUAD)
             put(packed, q, c, jnp.dot(pick[q], full, preferred_element_type=F32).astype(BF))
             start(di, di_own, d, c)
 
     for c in range(NC):
-        gz_done_gx_start(0, c)
-    for c in range(NC):
         pack(c)
+
+    def activated(block):
+        gate = jnp.minimum(block[:, : 2 * hid], 7.0)
+        up = jnp.clip(block[:, 2 * hid :], -7.0, 7.0)
+        return (up + 1.0) * gate * jax.nn.sigmoid(1.702 * gate)
+
+    slot = lax.rem(lax.broadcasted_iota(jnp.int32, (QUAD * SLOTS, 2 * hid), 0), SLOTS)
+
+    def give_back(c, d, rows_in=None):
+        q = lax.rem(quad + d, NS // QUAD)
+        block = lax.dot_general(
+            hidden[q] if rows_in is None else rows_in,
+            w_down[cols(c, 1), :],
+            (((1,), (1,)), ((), ())),
+            preferred_element_type=F32,
+        )
+        put(outgoing, q, c, block.astype(BF))
 
     for c in range(NC):
         for copy in weights[c][0]:
             copy.wait()
         for copy in weights[c][1][:4]:
             copy.wait_recv()
+        if c == NC - 1:
+            for copy in weights[0][1][4:]:
+                copy.wait_recv()
         for d in (0, 1, 3, 2):
             q = lax.rem(quad + d, NS // QUAD)
             wait(di, di_own, d, c)
             x = jnp.concatenate([arrived[q * QUAD + j, :, cols(c)] for j in range(QUAD)], 0)
             add = jnp.dot(x, w_in[cols(c), :], preferred_element_type=F32)
-            if c:
+            if c == 0:
+                acc[q] = add
+            elif c < NC - 1:
                 acc[q] += add
             else:
-                acc[q] = add
-
-    def activated(block):
-        gate = jnp.minimum(block[:, : 2 * hid], 7.0)
-        up = jnp.clip(block[:, 2 * hid :], -7.0, 7.0)
-        return (up + 1.0) * gate * jax.nn.sigmoid(1.702 * gate)
-
-    slot = lax.rem(lax.broadcasted_iota(jnp.int32, (QUAD * SLOTS, 2 * hid), 0), SLOTS)
-    for q in range(NS // QUAD):
-        first = jnp.where(slot < CAP, activated(acc[q, :, : 4 * hid]), 0.0)
-        second = jnp.where(slot >= CAP, activated(acc[q, :, 4 * hid :]), 0.0)
-        hidden[q] = jnp.concatenate([first, second], 1).astype(BF)
-
-    def give_back(c):
-        for copy in weights[c][1][4:]:
-            copy.wait_recv()
-        for d in (2, 1, 3, 0):
-            q = lax.rem(quad + d, NS // QUAD)
-            block = lax.dot_general(
-                hidden[q],
-                w_down[cols(c), :],
-                (((1,), (1,)), ((), ())),
-                preferred_element_type=F32,
-            )
-            put(outgoing, q, c, block.astype(BF))
-            start(re, re_own, d, c)
+                full = acc[q] + add
+                first = jnp.where(slot < CAP, activated(full[:, : 4 * hid]), 0.0)
+                second = jnp.where(slot >= CAP, activated(full[:, 4 * hid :]), 0.0)
+                units = jnp.concatenate([first, second], 1).astype(BF)
+                hidden[q] = units
+                give_back(0, d, units)
+                start(re, re_own, d, 0)
 
     def combine(c):
         sum_ = None
         for d in (0, 1, 3, 2):
             q = lax.rem(quad + d, NS // QUAD)
             wait(re, re_own, d, c)
-            y = jnp.concatenate([returned[q * QUAD + j, :, cols(c)] for j in range(QUAD)], 0)
+            y = jnp.concatenate([returned[q * QUAD + j, :, cols(c, 1)] for j in range(QUAD)], 0)
             add = jnp.dot(comb[q], y, preferred_element_type=F32)
             sum_ = add if sum_ is None else sum_ + add
-        moe_part[:, :, :, cols(c)] = sum_.astype(BF).reshape(NZ, 2, rows, CHUNKS[c][1])
+        moe_part[:, :, :, cols(c, 1)] = sum_.astype(BF).reshape(NZ, 2, rows, CHUNKS[1][c][1])
         ez_start(c)
 
     def finish_rows(c):
         ex(c).wait_recv()
         mine = slice(None) if c < NC_BOTH else xh
-        both = pair[mine, :, cols(c)].astype(F32) + pair_in[mine, :, cols(c)].astype(F32)
-        done = mixed[mine, :, cols(c)].astype(F32) + both
-        result[z, mine, :, cols(c)] = done.astype(BF)
+        both = pair[mine, :, cols(c, 1)].astype(F32) + pair_in[mine, :, cols(c, 1)].astype(F32)
+        done = mixed[mine, :, cols(c, 1)].astype(F32) + both
+        result[z, mine, :, cols(c, 1)] = done.astype(BF)
         gz_start(1, c)
 
     def write_out(c):
         if c < NC_BOTH:
-            gz_wait(1, c)
+            gz_all(1, c).wait_recv()
         else:
             gx(1, c, 1 - xh).wait_recv()
-        out_ref[cols(c), :] = result[:, :, :, cols(c)].reshape(tok, CHUNKS[c][1]).T
-
-    give_back(0)
-    give_back(1)
+        out_ref[cols(c, 1), :] = result[:, :, :, cols(c, 1)].reshape(tok, CHUNKS[1][c][1]).T
+
+    def prepare(c):
+        for copy in weights[c][1][4:]:
+            copy.wait_recv()
+        for d in (2, 1, 3, 0):
+            give_back(c, d)
+
+    def send_back(c):
+        for d in (2, 1, 3, 0):
+            start(re, re_own, d, c)
+
+    prepare(1)
+    send_back(1)
     mixed_across(1 - xh).wait_recv()
     for c in range(NC):
+        if c + 2 < NC:
+            prepare(c + 2)
         combine(c)
-        if c:
+        if c + 2 < NC:
+            send_back(c + 2)
+        if c >= 2:
+            finish_rows(c - 2)
+        if c == NC - 1:
             finish_rows(c - 1)
         ez_done_ex_start(c)
-        if c + 2 < NC:
-            give_back(c + 2)
     finish_rows(NC - 1)
     for c in range(NC):
         if c >= NC_BOTH:
-            gz_done_gx_start(1, c)
+            gz_all(1, c).wait_recv()
+            gx(1, c, xh).start()
         else:
             write_out(c)
     for c in range(NC_BOTH, NC):
@@ -636,7 +657,7 @@
     )(
         queries,
         sink_logits.reshape(1, -1),
-        norm_gain.reshape(1, width),
+        norm_gain,
         expert_ids.T,
         route_gates.T,
         key_rows,

time: 213 us -> 202 us (0.948); the launches traced: 213 us -> 200 us
  Pallas kernels: 209 us -> 197 us
    pallas_call x1, Pallas kernels: 209 us -> 197 us  [on_device(): pl.pallas_call(layer_kernel, out_shape=jax.ShapeDtypeStruct((width, tok),...]
where the time goes in v4:
time: 202 us; the launch traced here: 200 us
  Pallas kernels  197 us (98%)
  local copies, waits for them, and re-layouts  2.58 us (1%)
    pallas_call x1, Pallas kernels, on_device(): pl.pallas_call(layer_kernel, out_shape=jax.ShapeDtypeStruct((width, tok),...  197 us

profile of v4, /device:TPU:33, one launch (start us, length us, event | category | flops | bytes accessed | tf_op | source)
XLA Modules:
  0.0 199.8 jit_solution(1538346335751508664)
XLA Ops:
  0.0 197.2 %shard_map.118 = bf16[2880,256]{1,0:T(8,128)(2,1)} custom-call(bf16[256,256]{1,0:T(8,128)(2,1)} %query_ref.1, f32[1,4]{1,0:T(1,128)} %bitcast.13, f32[2880]{0:T(1024)} %gain_ref.1, s32[4,256]{1,0:T(4,128)} %bitcast.11, f32[4,256]{1,0:T(4,128)} %bitcast.12, bf16[256,512]{1,0:T(8,128)(2,1)} %key_ref.1, bf16[256,512]{1,0:T(8,128)(2,1)} %value_ref.1, ...), custom_call_target="tpu_custom_call" | custom-call | tf_op jit(solution)/shard_map/pallas_call | solution.py:619
  197.2 2.6 %copy.14 = bf16[256,2880]{0,1:T(8,128)(2,1)} copy(bf16[256,2880]{0,1:T(8,128)(2,1)} %bitcast.7) | data formatting | bytes 2949120

commit v5 on v4

--- a/solution.py
+++ b/solution.py
@@ -538,6 +538,10 @@
             gx(1, c, 1 - xh).wait_recv()
         out_ref[cols(c, 1), :] = result[:, :, :, cols(c, 1)].reshape(tok, CHUNKS[1][c][1]).T
 
+    def across_next(c):
+        gz_all(1, c).wait_recv()
+        gx(1, c, xh).start()
+
     def prepare(c):
         for copy in weights[c][1][4:]:
             copy.wait_recv()
@@ -561,15 +565,16 @@
             finish_rows(c - 2)
         if c == NC - 1:
             finish_rows(c - 1)
+            across_next(NC_BOTH)
+            write_out(0)
         ez_done_ex_start(c)
+    across_next(NC_BOTH + 1)
     finish_rows(NC - 1)
-    for c in range(NC):
-        if c >= NC_BOTH:
-            gz_all(1, c).wait_recv()
-            gx(1, c, xh).start()
-        else:
-            write_out(c)
-    for c in range(NC_BOTH, NC):
+    for c in range(1, NC_BOTH + 1):
+        write_out(c)
+    for c in range(NC_BOTH + 2, NC):
+        across_next(c)
+    for c in range(NC_BOTH + 1, NC):
         write_out(c)
 
     mixed_across(xh).wait_send()

time: 202 us -> 201 us (level)
  no operation moved by 1% of the time
where the time goes in v5:
time: 201 us; the launch traced here: 200 us
  Pallas kernels  197 us (98%)
  local copies, waits for them, and re-layouts  2.58 us (1%)
    pallas_call x1, Pallas kernels, on_device(): pl.pallas_call(layer_kernel, out_shape=jax.ShapeDtypeStruct((width, tok),...  197 us

profile of v5, /device:TPU:33, one launch (start us, length us, event | category | flops | bytes accessed | tf_op | source)
XLA Modules:
  0.0 199.6 jit_solution(18020099480549277563)
XLA Ops:
  0.0 197.0 %shard_map.118 = bf16[2880,256]{1,0:T(8,128)(2,1)} custom-call(bf16[256,256]{1,0:T(8,128)(2,1)} %query_ref.1, f32[1,4]{1,0:T(1,128)} %bitcast.13, f32[2880]{0:T(1024)} %gain_ref.1, s32[4,256]{1,0:T(4,128)} %bitcast.11, f32[4,256]{1,0:T(4,128)} %bitcast.12, bf16[256,512]{1,0:T(8,128)(2,1)} %key_ref.1, bf16[256,512]{1,0:T(8,128)(2,1)} %value_ref.1, ...), custom_call_target="tpu_custom_call" | custom-call | tf_op jit(solution)/shard_map/pallas_call | solution.py:624
  197.1 2.6 %copy.14 = bf16[256,2880]{0,1:T(8,128)(2,1)} copy(bf16[256,2880]{0,1:T(8,128)(2,1)} %bitcast.7) | data formatting | bytes 2949120
